TPU v7x, 128 devices: a whole 4x4x4 slice. The times are simulated.
128 devices in a mesh: row: 8 (over x_hi, y), col: 16 (over z, x_lo, core).
Axes of the slice: x: 4 (x_hi: 2, x_lo: 2; x = x_hi * 2 + x_lo), y: 4, z: 4, core: 2. Of those that a mesh axis runs over, the one named last changes fastest.
Arguments:
- velocity: float32 [3, 16, 16, 36, 32, 512], P(None, 'col', 'row'), may hold values from -6 to 6
- y_sizes: int32 [16], replicated, may hold values from 1 to 36, 512 in all
- old_place: int32 [16, 16], replicated, may hold values from 0 to 15, each once within a row
- new_col: int32 [16, 16], replicated, may hold values from 0 to 15, each once within a row
Outputs:
- divergence: float32 [16, 16, 2, 512, 512], P('row', 'col')
- peak: float32 [512, 512], replicated
Inputs may be any that keep to these rules, and one draw needn't show every extreme that they name: `y_sizes`: the heights sum to 512 and the tallest is exactly 36. `old_place`: each row is a permutation of 0 to 15. `new_col`: each row is a permutation of 0 to 16 - 1.
All inputs are finite; a program needn't handle non-finite values.
Results may differ from a plain program's by a relative error of at most 0.0003.
Values sent between devices are 32-bit elements; how exact they have to be, the bound alone decides.
A program may use at most 320 MiB of HBM per device.

v0:
```python
import math

import jax
import jax.numpy as jnp
from jax import lax
from jax.sharding import PartitionSpec as P

YMEAN = 32


EXACT = lax.Precision.HIGHEST


def items_in_groups(array, axis, split_dim, concat_dim, work, item_dim, out_dim):

    def moved(group):
        return lax.all_to_all(group, axis, split_axis=split_dim, concat_axis=concat_dim, tiled=True)

    items = jax.tree.leaves(array)[0].shape[item_dim]
    ends = [items * k // 2 for k in range(2 + 1)] if items % 2 == 0 else [0, items]
    groups = [
        jax.tree.map(lambda a: lax.slice_in_dim(a, low, high, axis=item_dim), array)
        for low, high in zip(ends, ends[1:])
    ]
    arrived = [moved(group) for group in groups]
    made = [work(group) for group in arrived]
    return jax.tree.map(lambda *parts: jnp.concatenate(parts, axis=out_dim), *made)


def source_rows(y_sizes, old_place, row_depth, height):
    ends = jnp.cumsum(y_sizes)
    starts = ends - y_sizes
    cells = jnp.arange(height, dtype=jnp.int32)
    block = jnp.sum((cells[:, None] >= ends[None, :]).astype(jnp.int32), axis=1)
    offset = cells - jnp.take(starts, block)
    return jnp.take(old_place, block, axis=1) * row_depth + offset


def spectral_matrix(positions, count):
    gap = (positions[:, None] - positions[None, :]) % count
    angle = gap.astype(jnp.float32) * (math.pi / count)
    parity = 1.0 - 2.0 * (gap % 2).astype(jnp.float32)
    divisor = jnp.where(gap == 0, 1.0, jnp.sin(angle))
    return jnp.where(gap == 0, 0.0, parity * jnp.cos(angle) / divisor * (2.0 / count))


def along_last(field, matrix):
    return jnp.dot(
        field, jnp.transpose(matrix), precision=EXACT, preferred_element_type=jnp.float32
    )


def along_rows(field, matrix):
    return jnp.einsum("jy,ksyx->ksjx", matrix, field, precision=EXACT)


def vertical_positions(slab_of, rows_count, columns, per_row, planes, thick):
    owner_row = jnp.arange(rows_count, dtype=jnp.int32)[:, None, None]
    owner_col = jnp.arange(columns, dtype=jnp.int32)[None, :, None]
    group = jnp.arange(per_row, dtype=jnp.int32)[None, None, :]
    zblock = owner_row * per_row + group
    slab = jnp.take(slab_of.reshape(-1), zblock * columns + owner_col)
    first = zblock * planes + slab * thick
    return (first[..., None] + jnp.arange(thick, dtype=jnp.int32)).reshape(-1)


def on_device(velocity, y_sizes, old_place, new_col):
    velocity = velocity[:, 0]
    row_depth = velocity.shape[2]
    planes = velocity.shape[3]
    x_cells = velocity.shape[4]
    places = velocity.shape[1]
    columns = lax.axis_size("col")
    rows_count = lax.axis_size("row")
    my_col = lax.axis_index("col")
    my_row = lax.axis_index("row")
    thick = planes // columns
    per_row = columns // rows_count
    blocks_y = y_sizes.shape[0]
    height = YMEAN * blocks_y
    hits = (new_col[:, :, None] == jnp.arange(columns, dtype=jnp.int32)[None, None, :]).astype(
        jnp.int32
    )
    slab_of = jnp.sum(hits * jnp.arange(columns, dtype=jnp.int32)[None, :, None], axis=1)
    rows_index = source_rows(y_sizes, old_place, row_depth, height)
    across_x = spectral_matrix(jnp.arange(x_cells, dtype=jnp.int32), x_cells)
    across_y = spectral_matrix(jnp.arange(height, dtype=jnp.int32), height)
    fields = velocity.shape[0]
    order = jnp.take(slab_of, my_col, axis=0)
    sliced = velocity.reshape(fields, places, row_depth, columns, thick, x_cells)
    outgoing = jnp.take(sliced, order, axis=3)
    settled = lax.all_to_all(
        lax.all_to_all(outgoing, "col", split_axis=3, concat_axis=3, tiled=True),
        "row",
        split_axis=3,
        concat_axis=1,
        tiled=True,
    )
    flat = settled.reshape(fields, blocks_y * row_depth, per_row, thick, x_cells)
    my_rows = lax.dynamic_slice_in_dim(rows_index, my_row * per_row, per_row, 0)
    pieces = []
    for group in range(per_row):
        picked = jnp.take(flat[:, :, group], my_rows[group], axis=1)
        pieces.append(jnp.swapaxes(picked, 1, 2))
    slabs = jnp.stack(pieces, axis=1)
    vertical = slabs[2]
    positions = vertical_positions(slab_of, rows_count, columns, per_row, planes, thick)
    across_z = spectral_matrix(positions, planes * columns)

    def turn(received):
        shape = received.shape
        slope = jnp.einsum(
            "ab,byx->ayx", across_z, received.reshape(-1, shape[3], shape[4]), precision=EXACT
        )
        return lax.all_to_all(
            slope.reshape(shape), ("row", "col"), split_axis=0, concat_axis=3, tiled=True
        )

    slope_z = items_in_groups(vertical[None], ("row", "col"), 3, 0, turn, 4, 4)[0]
    slope_x = along_last(slabs[0], across_x)
    field = slope_x + along_rows(slabs[1], across_y) + slope_z
    local_peak = jnp.max(jnp.abs(field), axis=(0, 1))
    peak = lax.pmax(local_peak, ("row", "col"))
    return (field[:, None], peak)


def solution(mesh):
    in_specs = (P(None, "col", "row", None, None, None), P(), P(), P())
    out_specs = (P("row", "col", None, None, None), P())
    return jax.shard_map(
        on_device, mesh=mesh, in_specs=in_specs, out_specs=out_specs, check_vma=False
    )
```

profile of v0, /device:TPU:1, one launch (start us, length us, event | category | flops | bytes accessed | tf_op | source)
XLA Modules:
  0.0 787.3 jit_solution(15811812712693186008)
XLA Ops:
  8.0 16.8 %reshape_squeeze.3 = f32[3,2,36,16,2,512]{5,4,3,2,1,0:T(2,128)} reshape(f32[3,1,2,36,32,512]{5,4,3,2,1,0:T(8,128)} %param.6) | data formatting | bytes 28311552 | tf_op jit(solution)/shard_map/reshape;squeeze | solution.py:90
  24.8 28.0 %gather_fusion = f32[16,3,2,36,2,512]{5,4,3,2,1,0:T(2,128)} fusion(f32[3,2,36,16,2,512]{5,4,3,2,1,0:T(2,128)} %reshape_squeeze.3, s32[1024]{0:T(1024)S(1)} %pad_clamp_fusion.3), kind=kCustom, calls=%fused_computation.2 | custom fusion | bytes 28311616 | tf_op jit(solution)/shard_map/jit(_take)/gather | solution.py:91
  52.9 9.4 %select_bitcast_fusion = f32[3,2,36,16,2,512]{5,4,2,1,0,3:T(2,128)S(1)} fusion(f32[16,3,2,36,2,512]{5,4,3,2,1,0:T(2,128)} %gather_fusion, pred[16]{0:T(512)(128)(4,1)S(1)} %compare_and_fusion.3), kind=kLoop, calls=%fused_computation.11 | loop fusion | flops 3538944 | bytes 28311568 | tf_op jit(solution)/shard_map/jit(_take)/select_n | solution.py:91
  62.3 163.4 %all_to_all.86 = f32[3,2,36,16,2,512]{5,4,2,1,0,3:T(2,128)} all-to-all(f32[3,2,36,16,2,512]{5,4,2,1,0,3:T(2,128)S(1)} %select_bitcast_fusion), channel_id=1, replica_groups=mesh['row'=8,'col'=16] {'col'}, dimensions={3} | all-to-all | bytes 28311552 | tf_op jit(solution)/shard_map/all_to_all | solution.py:93
  225.7 6.7 all-to-all-start.1
  234.6 10.1 %fusion.60 = (s32[512]{0:T(512)S(1)}, pred[512]{0:T(512)(128)(4,1)S(1)}) fusion(s32[512]{0:T(512)S(1)} %bitcast.145, s32[]{:T(128)} %bitcast.3, s32[]{:T(128)} %bitcast.4, s32[]{:T(128)} %bitcast.5, s32[]{:T(128)} %bitcast.6, s32[]{:T(128)} %bitcast.7, s32[]{:T(128)} %bitcast.8, s32[]{:T(128)} %bitcast.9, s32[]{:T(128)} %bitcast.10, s32[]{:T(128)} %bitcast.11, ...), kind=kLoop, calls=%fused_computation.115 | loop fusion | flops 19456 | bytes 6720 | tf_op jit(solution)/shard_map/sub | solution.py:35
  245.3 142.6 %all-to-all-done.1 = f32[3,2,36,16,2,512]{5,4,2,1,0,3:T(2,128)} async-done(((f32[3,2,36,16,2,512]{5,4,2,1,0,3:T(2,128)}), f32[3,2,36,16,2,512]{5,4,2,1,0,3:T(2,128)}, u32[]{:S(2)}, u32[]{:S(2)}) %all-to-all-start.1) | async-done | bytes 14155808 | tf_op jit(solution)/shard_map/all_to_all | solution.py:92
  387.9 8.2 %copy.85 = f32[3,8,2,36,2,2,512]{6,5,4,3,2,1,0:T(2,128)S(1)} copy(f32[3,8,2,36,2,2,512]{6,5,3,2,0,4,1:T(2,128)} %bitcast.26) | data formatting | bytes 28311552 | tf_op jit(solution)/shard_map/all_to_all | solution.py:92
  396.1 8.2 %slice_bitcast_fusion.1 = (f32[3,576,2,512]{3,2,1,0:T(2,128)}, f32[3,576,2,512]{3,2,1,0:T(2,128)}) fusion(f32[3,576,2,2,512]{4,3,2,1,0:T(2,128)S(1)} %bitcast.136), kind=kLoop, calls=%fused_computation.13 | loop fusion | bytes 28311552 | tf_op jit(solution)/shard_map/squeeze | solution.py:103
  404.3 19.8 %gather_fusion.3 = f32[512,3,2,512]{3,2,1,0:T(2,128)} fusion(f32[3,576,2,512]{3,2,1,0:T(2,128)} %get-tuple-element.30, s32[1024]{0:T(1024)S(1)} %pad_clamp_fusion.2), kind=kCustom, calls=%fused_computation.clone | custom fusion | bytes 12584960 | tf_op jit(solution)/shard_map/jit(_take)/gather | solution.py:103
  424.1 7.1 fusion.1
  431.3 20.3 %gather_fusion.4 = f32[512,3,2,512]{3,2,1,0:T(2,128)} fusion(f32[3,576,2,512]{3,2,1,0:T(2,128)} %get-tuple-element.31, s32[1024]{0:T(1024)S(1)} %pad_clamp_fusion.1), kind=kCustom, calls=%fused_computation.1.clone | custom fusion | bytes 12584960 | tf_op jit(solution)/shard_map/jit(_take)/gather | solution.py:103
  451.5 4.6 fusion
  459.5 2.9 copy.97
  462.4 7.0 all-to-all-start.4
  469.4 4.5 copy.93
  473.9 25.5 %all-to-all-done.4 = f32[1,2,2,512,256]{4,2,1,0,3:T(2,128)S(1)} async-done(((f32[1,2,2,512,256]{4,2,1,0,3:T(2,128)}), f32[1,2,2,512,256]{4,2,1,0,3:T(2,128)S(1)}, u32[]{:S(2)}, u32[]{:S(2)}) %all-to-all-start.4) | async-done | bytes 2097184 | tf_op jit(solution)/shard_map/all_to_all | solution.py:17
  500.8 4.8 all-to-all-start.2
  508.8 3.6 copy.119
  512.5 3.6 reshape.388
  516.1 10.0 %fusion.14 = f32[128,2,2,4,256]{4,0,3,2,1:T(8,128)S(1)} fusion(f32[512,4,256,1,1]{2,0,1,3,4:T(8,128)} %reshape.388, s32[512]{0:T(512)S(1)} %add.321, s32[128,2,2]{0,2,1:T(2,128)S(1)} %iota_add_fusion.2), kind=kOutput, calls=%fused_computation.30 | convolution fusion | flops 3230138368 | bytes 4198400 | tf_op jit(solution)/shard_map/ab,byx->ayx/dot_general | solution.py:112
  528.8 7.1 all-to-all-done.2
  535.9 6.4 all-to-all-start.5
  547.0 8.4 %fusion.16 = f32[128,2,2,4,256]{4,0,3,2,1:T(8,128)S(1)} fusion(f32[512,4,256,1,1]{2,0,1,3,4:T(8,128)S(1)} %reshape.387, s32[512]{0:T(512)S(1)} %add.321, s32[128,2,2]{0,2,1:T(2,128)S(1)} %iota_add_fusion.2), kind=kOutput, calls=%fused_computation.32 | convolution fusion | flops 3230138368 | bytes 4198400 | tf_op jit(solution)/shard_map/ab,byx->ayx/dot_general | solution.py:112
  558.1 13.9 %all-to-all-done.5 = f32[128,2,2,4,256]{4,3,2,1,0:T(4,128)} async-done(((f32[128,2,2,4,256]{4,3,2,1,0:T(4,128)}), f32[128,2,2,4,256]{4,3,2,1,0:T(4,128)}, u32[]{:S(2)}, u32[]{:S(2)}) %all-to-all-start.5) | async-done | bytes 2097184 | tf_op jit(solution)/shard_map/all_to_all | solution.py:115
  572.0 4.8 all-to-all-start.3
  577.0 15.6 %fusion.4 = f32[2,2,512,512]{3,2,1,0:T(8,128)} fusion(f32[3,1,2,512,512]{4,3,2,1,0:T(8,128)} %fusion.1, f32[3,1,2,512,512]{4,3,2,1,0:T(8,128)} %copy-done), kind=kOutput, calls=%fused_computation.20 | convolution fusion | flops 6452412416 | bytes 16777216 | tf_op jit(solution)/shard_map/dot_general | solution.py:48
  592.6 3.3 copy.100
  598.8 8.3 %all-to-all-done.3 = f32[128,2,2,4,256]{4,3,2,1,0:T(4,128)S(1)} async-done(((f32[128,2,2,4,256]{4,3,2,1,0:T(4,128)}), f32[128,2,2,4,256]{4,3,2,1,0:T(4,128)S(1)}, u32[]{:S(2)}, u32[]{:S(2)}) %all-to-all-start.3) | async-done | bytes 2097184 | tf_op jit(solution)/shard_map/all_to_all | solution.py:115
  608.8 3.3 all_to_all.72
  612.1 20.6 %abs_reduce_fusion = (f32[512,512]{1,0:T(8,128)}, f32[2,2,512,512]{3,2,1,0:T(8,128)}) fusion(f32[1,2,2,512,256]{4,3,2,1,0:T(8,128)S(1)} %copy-done.2, f32[1,2,2,512,256]{4,3,2,1,0:T(8,128)} %all_to_all.72, f32[2,2,512,512]{3,2,1,0:T(8,128)} %fusion.4, f32[3,1,2,512,512]{4,3,2,1,0:T(8,128)} %fusion.1, f32[3,1,2,512,512]{4,3,2,1,0:T(8,128)} %copy-done), kind=kOutput, calls=%fused_computation.27 | convolution fusion | flops 6457393152 | bytes 26214400 | tf_op jit(solution)/shard_map/jy,ksyx->ksjx/dot_general | solution.py:54
  632.7 145.3 %all-reduce.2.cloned.1.call-done = f32[512,512]{1,0:T(8,128)} async-done(((f32[512,512]{1,0:T(8,128)}), f32[512,512]{1,0:T(8,128)}) %all-reduce.2.cloned.1.call-update) | async-done | bytes 1048592 | tf_op jit(solution)/shard_map/pmax | solution.py:123
  (62 shorter events, 28.7 us)
Async XLA Ops:
  225.7 6.7 copy-start.3
  225.7 6.8 copy-start.4
  225.7 162.2 %all-to-all-start.1 = ((f32[3,2,36,16,2,512]{5,4,2,1,0,3:T(2,128)}), f32[3,2,36,16,2,512]{5,4,2,1,0,3:T(2,128)}, u32[]{:S(2)}, u32[]{:S(2)}) async-start(f32[3,2,36,16,2,512]{5,4,2,1,0,3:T(2,128)} %all_to_all.86), calls=%async_computation.1 | async-start | bytes 28311552 | tf_op jit(solution)/shard_map/all_to_all | solution.py:92
  451.5 4.6 slice-start
  451.5 4.7 slice-start.1
  456.2 3.3 copy-start
  462.4 37.0 %all-to-all-start.4 = ((f32[1,2,2,512,256]{4,2,1,0,3:T(2,128)}), f32[1,2,2,512,256]{4,2,1,0,3:T(2,128)S(1)}, u32[]{:S(2)}, u32[]{:S(2)}) async-start(f32[1,2,2,512,256]{4,2,1,0,3:T(2,128)} %copy.97), calls=%async_computation.4 | async-start | bytes 4194304 | tf_op jit(solution)/shard_map/all_to_all | solution.py:17
  499.5 1.3 copy-start.1
  500.8 35.1 %all-to-all-start.2 = ((f32[1,2,2,512,256]{4,2,1,0,3:T(2,128)}), f32[1,2,2,512,256]{4,2,1,0,3:T(2,128)S(1)}, u32[]{:S(2)}, u32[]{:S(2)}) async-start(f32[1,2,2,512,256]{4,2,1,0,3:T(2,128)} %copy.93), calls=%async_computation.2 | async-start | bytes 4194304 | tf_op jit(solution)/shard_map/all_to_all | solution.py:17
  535.9 36.1 %all-to-all-start.5 = ((f32[128,2,2,4,256]{4,3,2,1,0:T(4,128)}), f32[128,2,2,4,256]{4,3,2,1,0:T(4,128)}, u32[]{:S(2)}, u32[]{:S(2)}) async-start(f32[128,2,2,4,256]{4,3,2,1,0:T(4,128)} %copy.99), calls=%async_computation.5 | async-start | bytes 4194304 | tf_op jit(solution)/shard_map/all_to_all | solution.py:115
  572.0 35.1 %all-to-all-start.3 = ((f32[128,2,2,4,256]{4,3,2,1,0:T(4,128)}), f32[128,2,2,4,256]{4,3,2,1,0:T(4,128)S(1)}, u32[]{:S(2)}, u32[]{:S(2)}) async-start(f32[128,2,2,4,256]{4,3,2,1,0:T(4,128)} %copy.95), calls=%async_computation.3 | async-start | bytes 4194304 | tf_op jit(solution)/shard_map/all_to_all | solution.py:115
  576.8 201.2 %all-reduce.2.cloned.1.call-start = ((), (), s32[]{:S(2)}) async-start(), calls=%async_computation.6 | async-start | bytes 2097152 | tf_op jit(solution)/shard_map/pmax | solution.py:123
  608.8 3.3 copy-start.2
Sparse Core Ops, SparseCore 0:
  632.8 145.1 all-reduce.1
where the time goes:
time: 794 us; the launch traced here: 787 us
  waiting for transfers between devices  343 us (43%)
  blocking collectives  163 us (21%)
  local copies, waits for them, and re-layouts  147 us (19%)
  matrix products  54.7 us (7%)
  other arithmetic  35 us (4%)
  starting transfers between devices  29.9 us (4%)
  between operations  14.6 us (2%)
    all_to_all x1, blocking collectives, on_device(): lax.all_to_all(outgoing, 'col', split_axis=3, concat_axis=3, tiled=True)  163 us
    pmax x1, waiting for transfers between devices, on_device(): peak = lax.pmax(local_peak, ('row', 'col'))  145 us
    all_to_all x1, waiting for transfers between devices, on_device(): lax.all_to_all(lax.all_to_all(outgoing, 'col', split_axis=3, concat_axis=...  143 us
    gather x2, local copies, waits for them, and re-layouts, on_device(): picked = jnp.take(flat[:, :, group], my_rows[group], axis=1)  40.1 us
    all_to_all x2, waiting for transfers between devices, moved(): lax.all_to_all(group, axis, split_axis=split_dim, concat_axis=concat_dim,...  32.6 us
    gather x1, local copies, waits for them, and re-layouts, on_device(): outgoing = jnp.take(sliced, order, axis=3)  28 us
    all_to_all x2, waiting for transfers between devices, turn(): lax.all_to_all(slope.reshape(shape), ('row', 'col'), split_axis=0, concat...  22.2 us
    dot_general x1, matrix products, along_rows(): return jnp.einsum('jy,ksyx->ksjx', matrix, field, precision=EXACT)  20.6 us
  transfers between devices with their start and end apart: 6, of which 6 were waited for; matrix products, arithmetic and copies ran while one was open for 10% of the time, Pallas kernels for 0%

commit v1 on v0

v1 whole, which is shorter than its diff:
```python
import functools
import math

import jax
import jax.numpy as jnp
import numpy as np
from jax import lax
from jax.experimental import pallas as pl
from jax.experimental.pallas import tpu as pltpu
from jax.sharding import PartitionSpec as P

BOTH = ("row", "col")


def spectral_matrix(count):
    gap = (np.arange(count)[:, None] - np.arange(count)[None, :]) % count
    angle = gap.astype(np.float64) * (math.pi / count)
    parity = 1.0 - 2.0 * (gap % 2)
    divisor = np.where(gap == 0, 1.0, np.sin(angle))
    return np.where(gap == 0, 0.0, parity * np.cos(angle) / divisor * (2.0 / count))


def two_halves(matrix):
    high = matrix.astype(np.float32).astype(jnp.bfloat16)
    low = (matrix - high.astype(np.float64)).astype(np.float32).astype(jnp.bfloat16)
    return jnp.asarray(high), jnp.asarray(low)


def split(value):
    high = value.astype(jnp.bfloat16)
    return high, (value - high.astype(jnp.float32)).astype(jnp.bfloat16)


def dot(a, b):
    return jnp.dot(a, b, preferred_element_type=jnp.float32)


def prepare_kernel(v_ref, high_ref, low_ref, out_ref):
    rows, planes, width = v_ref.shape[1:]
    parts = out_ref.shape[0]
    flat = out_ref.reshape(parts * rows, out_ref.shape[2])

    def emit(piece):
        for row in range(rows):
            value = piece(row)
            stacked = jnp.concatenate(
                [value[:, q * parts : (q + 1) * parts] for q in range(width // parts)], axis=0
            )
            flat[pl.ds(row, parts, stride=rows), :] = stacked.T

    @pl.when(pl.program_id(0) == 0)
    def _():
        high, low = split(v_ref[0].reshape(rows * planes, width))
        slope = dot(high, high_ref[...]) + (dot(high, low_ref[...]) + dot(low, high_ref[...]))
        emit(lambda row: slope[row * planes : (row + 1) * planes])

    @pl.when(pl.program_id(0) != 0)
    def _():
        emit(lambda row: v_ref[0, row])


def prepare(velocity, high, low, parts):
    fields, rows, planes, width = velocity.shape
    lanes = planes * width // parts
    groups = rows // 8
    whole = pl.BlockSpec((width, width), lambda f, g: (0, 0))
    return pl.pallas_call(
        prepare_kernel,
        grid=(fields, groups),
        in_specs=[pl.BlockSpec((1, 8, planes, width), lambda f, g: (f, g, 0, 0)), whole, whole],
        out_specs=pl.BlockSpec((parts, 8, lanes), lambda f, g: (0, f * groups + g, 0)),
        out_shape=jax.ShapeDtypeStruct((parts, fields * rows, lanes), jnp.float32),
        compiler_params=pltpu.CompilerParams(vmem_limit_bytes=48 << 20),
        cost_estimate=pl.CostEstimate(
            flops=6 * rows * planes * width * width,
            bytes_accessed=8 * fields * rows * planes * width,
            transcendentals=0,
        ),
        name="prepare",
    )(velocity, high, low)


def middle_kernel(
    sizes_ref, place_ref, col_ref, r_ref, high_ref, low_ref, out_ref,
    aligned, v_high, v_low, total, field, peaks,
):
    step = pl.program_id(0)
    blocks = place_ref.shape[1]
    depth = r_ref.shape[2] // 6
    height = field.shape[1]
    zblocks = place_ref.shape[0]
    planes = field.shape[0] // zblocks
    quarters = total.shape[0]
    lanes = r_ref.shape[3]
    chunks = height // lanes

    @pl.when(step < zblocks)
    def _():
        start = 0
        for b in range(blocks):
            place = place_ref[step, b]
            for f in range(3):
                aligned[f, pl.ds(start, depth), :] = r_ref[
                    place // 2, 0, pl.ds(2 * depth * f + depth * (place % 2), depth), :
                ]
            start = start + sizes_ref[b]
        high, low = split(aligned[1, :height, :])
        slope = dot(high_ref[...], high) + (dot(low_ref[...], high) + dot(high_ref[...], low))
        slope = (slope + aligned[0, :height, :]).T
        vertical = aligned[2, :height, :].T
        high, low = split(vertical)
        at = pl.multiple_of(step * planes, planes)
        for q in range(quarters):
            rows = slice(q * planes, (q + 1) * planes)
            total[q, pl.ds(at, planes), :] = slope[rows]
            v_high[q, pl.ds(at, planes), :] = high[rows]
            v_low[q, pl.ds(at, planes), :] = low[rows]

    @pl.when((step >= zblocks) & (step < zblocks + quarters))
    def _():
        q = step - zblocks
        value = total[q] + (
            dot(high_ref[...], v_high[q])
            + (dot(low_ref[...], v_high[q]) + dot(high_ref[...], v_low[q]))
        )
        field[...] = value
        top = jnp.max(jnp.abs(value), axis=0, keepdims=True)
        for chunk in range(chunks):
            peaks[pl.ds(q * chunks + chunk, 1), :] = top[:, chunk * lanes : (chunk + 1) * lanes]
        slabs = col_ref.shape[1]
        for zblock in range(zblocks):
            for slab in range(slabs):
                target = (zblock // 2) * slabs + col_ref[zblock, slab]
                low_row = zblock * planes + 2 * slab
                for chunk in range(chunks):
                    at = 4 * chunk + 2 * (zblock % 2)
                    out_ref[target, at : at + 2, :] = field[
                        low_row : low_row + 2, chunk * lanes : (chunk + 1) * lanes
                    ]

    @pl.when(step == zblocks + quarters)
    def _():
        out_ref[...] = jnp.broadcast_to(peaks[...][None], out_ref.shape)


def middle(received, sizes, old_place, new_col, high, low):
    rows, cols, depth, lanes = received.shape
    zblocks = old_place.shape[0]
    height = high.shape[0]
    parts = rows * cols
    quarters = 4
    whole = pl.BlockSpec(high.shape, lambda i: (0, 0))
    smem = pl.BlockSpec(memory_space=pltpu.SMEM)
    return pl.pallas_call(
        middle_kernel,
        grid=(zblocks + quarters + 1,),
        in_specs=[
            smem,
            smem,
            smem,
            pl.BlockSpec(
                (rows, 1, depth, lanes), lambda i: (0, jnp.minimum(i, zblocks - 1), 0, 0)
            ),
            whole,
            whole,
        ],
        out_specs=pl.BlockSpec(
            (parts, 16, lanes), lambda i: (0, jnp.maximum(i - zblocks, 0), 0)
        ),
        out_shape=jax.ShapeDtypeStruct((parts, 16 * (quarters + 1), lanes), jnp.float32),
        scratch_shapes=[
            pltpu.VMEM((3, height + 40, lanes), jnp.float32),
            pltpu.VMEM((quarters, height, height), jnp.bfloat16),
            pltpu.VMEM((quarters, height, height), jnp.bfloat16),
            pltpu.VMEM((quarters, height, height), jnp.float32),
            pltpu.VMEM((height, height), jnp.float32),
            pltpu.VMEM((16, lanes), jnp.float32),
        ],
        compiler_params=pltpu.CompilerParams(vmem_limit_bytes=56 << 20),
        cost_estimate=pl.CostEstimate(
            flops=48 * height**3, bytes_accessed=20 << 20, transcendentals=0
        ),
        name="middle",
    )(sizes, old_place, new_col, received, high, low)


def finish_kernel(g_ref, p_ref, out_ref, peak_ref):
    parts, rows, lanes = g_ref.shape
    flat = g_ref.reshape(parts * rows, lanes)
    tops = p_ref.reshape(parts * rows, lanes)
    thick = out_ref.shape[0]
    chunks = rows // thick
    q = pl.program_id(0)
    for chunk in range(chunks):
        ys = slice(chunk * lanes, (chunk + 1) * lanes)
        for plane in range(thick):
            out_ref[plane, ys, :] = flat[pl.ds(chunk * thick + plane, parts, stride=rows), :].T
        peak_ref[ys, :] = tops[pl.ds(q * chunks + chunk, parts, stride=rows), :].T


def finish(received, thick, height):
    parts, rows, lanes = received.shape
    quarters = rows // 16 - 1
    return pl.pallas_call(
        finish_kernel,
        grid=(quarters,),
        in_specs=[
            pl.BlockSpec((parts, 16, lanes), lambda q: (0, q, 0)),
            pl.BlockSpec((parts, 16, lanes), lambda q: (0, quarters, 0)),
        ],
        out_specs=[
            pl.BlockSpec((thick, height, parts), lambda q: (0, 0, q)),
            pl.BlockSpec((height, parts), lambda q: (0, q)),
        ],
        out_shape=[
            jax.ShapeDtypeStruct((thick, height, quarters * parts), jnp.float32),
            jax.ShapeDtypeStruct((height, quarters * parts), jnp.float32),
        ],
        compiler_params=pltpu.CompilerParams(vmem_limit_bytes=48 << 20),
        cost_estimate=pl.CostEstimate(flops=1 << 20, bytes_accessed=10 << 20, transcendentals=0),
        name="finish",
    )(received, received)


def exchange(blocks):
    return lax.all_to_all(blocks, BOTH, split_axis=0, concat_axis=0, tiled=True)


def on_device(velocity, y_sizes, old_place, new_col):
    fields, _, places, depth, planes, width = velocity.shape
    rows, cols = lax.axis_size("row"), lax.axis_size("col")
    parts = rows * cols
    matrix = spectral_matrix(width)
    high, low = two_halves(matrix)
    high_t, low_t = two_halves(matrix.T)
    outgoing = prepare(
        velocity.reshape(fields, places * depth, planes, width), high_t, low_t, parts
    )
    arrived = exchange(outgoing).reshape(rows, cols, fields * places * depth, parts)
    shares = middle(arrived, y_sizes, old_place, new_col, high, low)
    field, peak = finish(exchange(shares), 4, width)
    return field.reshape(2, 1, 2, width, width), peak


def solution(mesh):
    in_specs = (P(None, "col", "row", None, None, None), P(), P(), P())
    out_specs = (P("row", "col", None, None, None), P())
    return jax.shard_map(
        on_device, mesh=mesh, in_specs=in_specs, out_specs=out_specs, check_vma=False
    )
```

time: 794 us -> 303 us (0.38)
  waiting for transfers between devices: 343 us -> 0 us
  local copies, waits for them, and re-layouts: 147 us -> 2.08 us
  blocking collectives: 163 us -> 247 us
  matrix products: 54.7 us -> 0 us
  Pallas kernels: 0 us -> 52.9 us
  other arithmetic: 35 us -> 0 us
  starting transfers between devices: 29.9 us -> 0 us
  between operations: 14.6 us -> 0.64 us
    all_to_all x5 -> x0, waiting for transfers between devices: 197 us -> none  [the longest x1 143 us: on_device(): lax.all_to_all(lax.all_to_all(outgoing, 'col', split_axis=3, concat_axis=...]
    pmax x1 -> x0, waiting for transfers between devices: 145 us -> none  [on_device(): peak = lax.pmax(local_peak, ('row', 'col'))]
    all_to_all x1 -> x2, blocking collectives: 163 us -> 247 us  [exchange(): return lax.all_to_all(blocks, BOTH, split_axis=0, concat_axis=0, tiled=True)]
    gather x8 -> x0, local copies, waits for them, and re-layouts: 72.1 us -> none  [the longest x2 40.1 us: on_device(): picked = jnp.take(flat[:, :, group], my_rows[group], axis=1)]
    dot_general x4 -> x0, matrix products: 54.7 us -> none  [the longest x1 20.6 us: along_rows(): return jnp.einsum('jy,ksyx->ksjx', matrix, field, precision=EXACT)]
    pallas_call x0 -> x3, Pallas kernels: none -> 52.9 us  [the longest x1 25.1 us: middle(): pl.pallas_call(middle_kernel, grid=(zblocks + quarters + 1,), in_specs=[s...]
    all_to_all x5 -> x0, starting transfers between devices: 29.7 us -> none  [the longest x2 11.8 us: moved(): lax.all_to_all(group, axis, split_axis=split_dim, concat_axis=concat_dim,...]
    all_to_all x7 -> x0, local copies, waits for them, and re-layouts: 25.1 us -> none  [the longest x4 11.2 us: turn(): lax.all_to_all(slope.reshape(shape), ('row', 'col'), split_axis=0, concat...]
  transfers between devices with their start and end apart: 6 -> 0, of which waited for: 6 -> 0; matrix products, arithmetic and copies ran while one was open for 10% -> 0% of each run, Pallas kernels for 0% -> 0%
where the time goes in v1:
time: 303 us; the launch traced here: 302 us
  blocking collectives  247 us (82%)
  Pallas kernels  52.9 us (17%)
    all_to_all x2, blocking collectives, exchange(): return lax.all_to_all(blocks, BOTH, split_axis=0, concat_axis=0, tiled=True)  247 us
    pallas_call x1, Pallas kernels, middle(): pl.pallas_call(middle_kernel, grid=(zblocks + quarters + 1,), in_specs=[s...  25.1 us
    pallas_call x1, Pallas kernels, prepare(): pl.pallas_call(prepare_kernel, grid=(fields, groups), in_specs=[pl.BlockS...  24 us

profile of v1, /device:TPU:1, one launch (start us, length us, event | category | flops | bytes accessed | tf_op | source)
XLA Modules:
  0.0 302.2 jit_solution(8058963488735959734)
XLA Ops:
  0.6 0.0 copy-start
  0.6 1.0 copy-done
  1.7 0.0 copy-start.1
  1.7 1.0 copy-done.1
  2.7 24.0 %prepare.1 = f32[128,216,128]{2,1,0:T(8,128)} custom-call(f32[3,72,32,512]{3,2,1,0:T(8,128)} %bitcast.5, bf16[512,512]{1,0:T(8,128)(2,1)S(1)} %copy-done.1, bf16[512,512]{1,0:T(8,128)(2,1)S(1)} %copy-done), custom_call_target="tpu_custom_call" | custom-call | flops 3623878656 | bytes 28311552 | tf_op jit(solution)/shard_map/prepare/pallas_call | solution.py:67
  26.7 174.0 %all_to_all.10 = f32[128,216,128]{2,1,0:T(8,128)} all-to-all(f32[128,216,128]{2,1,0:T(8,128)} %prepare.1), channel_id=1, replica_groups=mesh['row'=8,'col'=16] {'row','col'}, dimensions={0} | all-to-all | bytes 28311552 | tf_op jit(solution)/shard_map/all_to_all | solution.py:226
  200.7 25.1 %middle.1 = f32[128,80,128]{2,1,0:T(8,128)} custom-call(s32[16]{0:T(128)} %sizes_ref.1, s32[16,16]{1,0:T(8,128)} %place_ref.1, s32[16,16]{1,0:T(8,128)} %col_ref.1, f32[8,16,216,128]{3,2,1,0:T(8,128)} %bitcast.6, bf16[512,512]{1,0:T(8,128)(2,1)} %constant.8.clone.high_ref, bf16[512,512]{1,0:T(8,128)(2,1)} %constant.9.clone.low_ref), custom_call_target="tpu_custom_call" | custom-call | flops 6442450944 | bytes 20971520 | tf_op jit(solution)/shard_map/middle/pallas_call | solution.py:154
  225.8 72.6 %all_to_all.11.g_ref.p_ref = f32[128,80,128]{2,1,0:T(8,128)S(1)} all-to-all(f32[128,80,128]{2,1,0:T(8,128)} %middle.1), channel_id=1, replica_groups=mesh['row'=8,'col'=16] {'row','col'}, dimensions={0} | all-to-all | bytes 10485760 | tf_op jit(solution)/shard_map/all_to_all | solution.py:226
  298.4 3.8 %finish.1 = (f32[4,512,512]{2,1,0:T(8,128)}, f32[512,512]{1,0:T(8,128)}) custom-call(f32[128,80,128]{2,1,0:T(8,128)S(1)} %all_to_all.11.g_ref.p_ref, f32[128,80,128]{2,1,0:T(8,128)S(1)} %all_to_all.11.g_ref.p_ref), custom_call_target="tpu_custom_call" | custom-call | flops 1048576 | bytes 10485760 | tf_op jit(solution)/shard_map/finish/pallas_call | solution.py:204
Async XLA Ops:
  0.6 1.0 copy-start
  1.7 1.0 copy-start.1

commit v2 on v1

--- a/solution.py
+++ b/solution.py
@@ -35,48 +35,121 @@
     return jnp.dot(a, b, preferred_element_type=jnp.float32)
 
 
-def prepare_kernel(v_ref, high_ref, low_ref, out_ref):
-    rows, planes, width = v_ref.shape[1:]
-    parts = out_ref.shape[0]
-    flat = out_ref.reshape(parts * rows, out_ref.shape[2])
-
-    def emit(piece):
-        for row in range(rows):
-            value = piece(row)
+def spread_kernel(
+    v_ref, high_ref, low_ref, out_ref, stage, send, in_sems, send_sem, recv_sem, own_sem
+):
+    fields, rows, planes, width = v_ref.shape
+    parts, _, lanes = out_ref.shape
+    chunk = send.shape[1] // parts
+    per_field = rows // 8
+    groups = fields * per_field
+    per_chunk = chunk // 8
+    slots = stage.shape[0]
+    row, col = lax.axis_index("row"), lax.axis_index("col")
+    me = row * 16 + col
+    x, y, z, core = (row // 4) * 2 + (col // 2) % 2, row % 4, col // 4, col % 2
+
+    def load(n):
+        return pltpu.make_async_copy(
+            v_ref.at[fields - 1 - n // per_field, pl.ds((n % per_field) * 8, 8)],
+            stage.at[n % slots],
+            in_sems.at[n % slots],
+        )
+
+    def post(j):
+        at = pl.ds(pl.multiple_of(j * chunk, 8), chunk)
+
+        def one(i, _):
+            offset = ((i + core * (parts - 2 * i)) * 37) % parts
+            there_x = (x + offset // 32) % 4
+            there_y = (y + (offset // 8) % 4) % 4
+            there_z = (z + (offset // 2) % 4) % 4
+            there_core = (core + offset % 2) % 2
+            to_row = (there_x // 2) * 4 + there_y
+            to_col = there_z * 4 + (there_x % 2) * 2 + there_core
+            part = to_row * 16 + to_col
+            pltpu.make_async_remote_copy(
+                src_ref=send.at[j, pl.ds(pl.multiple_of(part * chunk, 8), chunk)],
+                dst_ref=out_ref.at[me, at],
+                send_sem=send_sem,
+                recv_sem=recv_sem,
+                device_id=(to_row, to_col),
+                device_id_type=pl.DeviceIdType.MESH,
+            ).start()
+            return 0
+
+        lax.fori_loop(1, parts, one, 0)
+        pltpu.make_async_copy(
+            send.at[j, pl.ds(pl.multiple_of(me * chunk, 8), chunk)], out_ref.at[me, at], own_sem
+        ).start()
+
+    def group(n, slope_of):
+        load(n).wait()
+        value = slope_of(stage.at[n % slots])
+        for r in range(8):
+            piece = value(r)
             stacked = jnp.concatenate(
-                [value[:, q * parts : (q + 1) * parts] for q in range(width // parts)], axis=0
+                [piece[:, q * parts : (q + 1) * parts] for q in range(width // parts)], axis=0
             )
-            flat[pl.ds(row, parts, stride=rows), :] = stacked.T
-
-    @pl.when(pl.program_id(0) == 0)
-    def _():
-        high, low = split(v_ref[0].reshape(rows * planes, width))
+            at = pl.ds((n % per_chunk) * 8 + r, parts, stride=chunk)
+            send[n // per_chunk, at, :] = stacked.T
+
+        @pl.when(n + slots < groups)
+        def _():
+            load(n + slots).start()
+
+        @pl.when((n % per_chunk == 0) & (n > 0))
+        def _():
+            post(n // per_chunk - 1)
+
+        return 0
+
+    def plain(ref):
+        return lambda r: ref[r]
+
+    def along_x(ref):
+        high, low = split(ref[...].reshape(8 * planes, width))
         slope = dot(high, high_ref[...]) + (dot(high, low_ref[...]) + dot(low, high_ref[...]))
-        emit(lambda row: slope[row * planes : (row + 1) * planes])
-
-    @pl.when(pl.program_id(0) != 0)
-    def _():
-        emit(lambda row: v_ref[0, row])
-
-
-def prepare(velocity, high, low, parts):
+        return lambda r: slope[r * planes : (r + 1) * planes]
+
+    for n in range(slots):
+        load(n).start()
+    middle = (fields - 1) * per_field
+    lax.fori_loop(0, middle, lambda n, _: group(n, plain), 0)
+    lax.fori_loop(middle, groups, lambda n, _: group(n, along_x), 0)
+    post(groups // per_chunk - 1)
+    sent = out_ref.at[pl.ds(0, parts - 1)]
+    pltpu.make_async_copy(out_ref.at[me], out_ref.at[me], own_sem).wait()
+    pltpu.make_async_copy(sent, sent, send_sem).wait()
+    pltpu.make_async_copy(sent, sent, recv_sem).wait()
+
+
+def spread(velocity, high, low, parts):
     fields, rows, planes, width = velocity.shape
     lanes = planes * width // parts
-    groups = rows // 8
-    whole = pl.BlockSpec((width, width), lambda f, g: (0, 0))
+    chunk = 24
+    vmem = pl.BlockSpec(memory_space=pltpu.VMEM)
+    anywhere = pl.BlockSpec(memory_space=pl.ANY)
     return pl.pallas_call(
-        prepare_kernel,
-        grid=(fields, groups),
-        in_specs=[pl.BlockSpec((1, 8, planes, width), lambda f, g: (f, g, 0, 0)), whole, whole],
-        out_specs=pl.BlockSpec((parts, 8, lanes), lambda f, g: (0, f * groups + g, 0)),
+        spread_kernel,
+        in_specs=[anywhere, vmem, vmem],
+        out_specs=anywhere,
         out_shape=jax.ShapeDtypeStruct((parts, fields * rows, lanes), jnp.float32),
-        compiler_params=pltpu.CompilerParams(vmem_limit_bytes=48 << 20),
+        scratch_shapes=[
+            pltpu.VMEM((3, 8, planes, width), jnp.float32),
+            pltpu.VMEM((fields * rows // chunk, parts * chunk, lanes), jnp.float32),
+            pltpu.SemaphoreType.DMA((3,)),
+            pltpu.SemaphoreType.DMA,
+            pltpu.SemaphoreType.DMA,
+            pltpu.SemaphoreType.DMA,
+        ],
+        compiler_params=pltpu.CompilerParams(vmem_limit_bytes=48 << 20, has_side_effects=True),
         cost_estimate=pl.CostEstimate(
             flops=6 * rows * planes * width * width,
             bytes_accessed=8 * fields * rows * planes * width,
             transcendentals=0,
         ),
-        name="prepare",
+        name="spread",
     )(velocity, high, low)
 
 
@@ -106,8 +179,8 @@
             start = start + sizes_ref[b]
         high, low = split(aligned[1, :height, :])
         slope = dot(high_ref[...], high) + (dot(low_ref[...], high) + dot(high_ref[...], low))
-        slope = (slope + aligned[0, :height, :]).T
-        vertical = aligned[2, :height, :].T
+        slope = (slope + aligned[2, :height, :]).T
+        vertical = aligned[0, :height, :].T
         high, low = split(vertical)
         at = pl.multiple_of(step * planes, planes)
         for q in range(quarters):
@@ -233,10 +306,9 @@
     matrix = spectral_matrix(width)
     high, low = two_halves(matrix)
     high_t, low_t = two_halves(matrix.T)
-    outgoing = prepare(
+    arrived = spread(
         velocity.reshape(fields, places * depth, planes, width), high_t, low_t, parts
-    )
-    arrived = exchange(outgoing).reshape(rows, cols, fields * places * depth, parts)
+    ).reshape(rows, cols, fields * places * depth, parts)
     shares = middle(arrived, y_sizes, old_place, new_col, high, low)
     field, peak = finish(exchange(shares), 4, width)
     return field.reshape(2, 1, 2, width, width), peak

time: 303 us -> 275 us (0.908)
  blocking collectives: 247 us -> 69.2 us
  Pallas kernels: 52.9 us -> 202 us
    all_to_all x2 -> x1, blocking collectives: 247 us -> 69.2 us  [exchange(): return lax.all_to_all(blocks, BOTH, split_axis=0, concat_axis=0, tiled=True)]
    pallas_call x1, Pallas kernels: 24 us -> 173 us  [spread(): pl.pallas_call(spread_kernel, in_specs=[anywhere, vmem, vmem], out_specs=...]
where the time goes in v2:
time: 275 us; the launch traced here: 274 us
  Pallas kernels  202 us (73%)
  blocking collectives  69.2 us (25%)
    pallas_call x1, Pallas kernels, spread(): pl.pallas_call(spread_kernel, in_specs=[anywhere, vmem, vmem], out_specs=...  173 us
    all_to_all x1, blocking collectives, exchange(): return lax.all_to_all(blocks, BOTH, split_axis=0, concat_axis=0, tiled=True)  69.2 us
    pallas_call x1, Pallas kernels, middle(): pl.pallas_call(middle_kernel, grid=(zblocks + quarters + 1,), in_specs=[s...  25.2 us

profile of v2, /device:TPU:1, one launch (start us, length us, event | category | flops | bytes accessed | tf_op | source)
XLA Modules:
  0.0 274.2 jit_solution(11277839010121281868)
XLA Ops:
  0.6 0.0 copy-start
  0.6 1.0 copy-done
  1.7 0.0 copy-start.1
  1.7 1.0 copy-done.1
  2.7 173.3 %spread.1 = f32[128,216,128]{2,1,0:T(8,128)} custom-call(f32[3,72,32,512]{3,2,1,0:T(8,128)} %bitcast.5, bf16[512,512]{1,0:T(8,128)(2,1)S(1)} %copy-done.1, bf16[512,512]{1,0:T(8,128)(2,1)S(1)} %copy-done), custom_call_target="tpu_custom_call" | custom-call | flops 3623878656 | bytes 28311552 | tf_op jit(solution)/shard_map/spread/pallas_call | solution.py:133
  176.0 25.2 %middle.1 = f32[128,80,128]{2,1,0:T(8,128)} custom-call(s32[16]{0:T(128)} %sizes_ref.1, s32[16,16]{1,0:T(8,128)} %place_ref.1, s32[16,16]{1,0:T(8,128)} %col_ref.1, f32[8,16,216,128]{3,2,1,0:T(8,128)} %bitcast.6, bf16[512,512]{1,0:T(8,128)(2,1)} %constant.8.clone.high_ref, bf16[512,512]{1,0:T(8,128)(2,1)} %constant.9.clone.low_ref), custom_call_target="tpu_custom_call" | custom-call | flops 6442450944 | bytes 20971520 | tf_op jit(solution)/shard_map/middle/pallas_call | solution.py:227
  201.2 69.2 %all_to_all.5.g_ref.p_ref = f32[128,80,128]{2,1,0:T(8,128)S(1)} all-to-all(f32[128,80,128]{2,1,0:T(8,128)} %middle.1), channel_id=1, replica_groups=mesh['row'=8,'col'=16] {'row','col'}, dimensions={0} | all-to-all | bytes 10485760 | tf_op jit(solution)/shard_map/all_to_all | solution.py:299
  270.3 3.8 %finish.1 = (f32[4,512,512]{2,1,0:T(8,128)}, f32[512,512]{1,0:T(8,128)}) custom-call(f32[128,80,128]{2,1,0:T(8,128)S(1)} %all_to_all.5.g_ref.p_ref, f32[128,80,128]{2,1,0:T(8,128)S(1)} %all_to_all.5.g_ref.p_ref), custom_call_target="tpu_custom_call" | custom-call | flops 1048576 | bytes 10485760 | tf_op jit(solution)/shard_map/finish/pallas_call | solution.py:277
Async XLA Ops:
  0.6 1.0 copy-start
  1.7 1.0 copy-start.1

commit v3 on v2

v3 whole, which is shorter than its diff:
```python
import math

import jax
import jax.numpy as jnp
import numpy as np
from jax import lax
from jax.experimental import pallas as pl
from jax.experimental.pallas import tpu as pltpu
from jax.sharding import PartitionSpec as P


def spectral_matrix(count):
    gap = (np.arange(count)[:, None] - np.arange(count)[None, :]) % count
    angle = gap.astype(np.float64) * (math.pi / count)
    parity = 1.0 - 2.0 * (gap % 2)
    divisor = np.where(gap == 0, 1.0, np.sin(angle))
    return np.where(gap == 0, 0.0, parity * np.cos(angle) / divisor * (2.0 / count))


def two_halves(matrix):
    high = matrix.astype(np.float32).astype(jnp.bfloat16)
    low = (matrix - high.astype(np.float64)).astype(np.float32).astype(jnp.bfloat16)
    return jnp.asarray(high), jnp.asarray(low)


def split(value):
    high = value.astype(jnp.bfloat16)
    return high, (value - high.astype(jnp.float32)).astype(jnp.bfloat16)


def dot(a, b):
    return jnp.dot(a, b, preferred_element_type=jnp.float32)


def fused_kernel(
    v_ref, high_ref, low_ref, sizes_ref, place_ref, col_ref, out_ref,
    stage, send, in_z, in_y, in_x, aligned, v_high, v_low, total, field, shares, peaks,
    ends, bounds, source, slab_of,
    in_sems, send_sem, recv_sems, share_send_sem, share_recv_sems, own_sem,
):
    fields, rows, planes, width = v_ref.shape
    lanes = send.shape[2]
    parts = lanes
    chunk = send.shape[1] // parts
    per_field = rows // 8
    groups = fields * per_field
    per_chunk = chunk // 8
    chunks_per_field = rows // chunk
    slots = stage.shape[0]
    quarters = total.shape[0]
    height = total.shape[2]
    pieces = height // lanes
    zblocks, blocks = place_ref.shape
    depth = rows // 2
    pad = (in_z.shape[0] - parts * rows) // 2
    arrivals = (in_z, in_y, in_x)
    row, col = lax.axis_index("row"), lax.axis_index("col")
    me = row * 16 + col
    x, y, z, core = (row // 4) * 2 + (col // 2) % 2, row % 4, col // 4, col % 2

    def load(n):
        return pltpu.make_async_copy(
            v_ref.at[fields - 1 - n // per_field, pl.ds((n % per_field) * 8, 8)],
            stage.at[n % slots],
            in_sems.at[n % slots],
        )

    def to_all(copy):
        def one(i, _):
            offset = ((i + core * (parts - 2 * i)) * 37) % parts
            there_x = (x + offset // 32) % 4
            there_y = (y + (offset // 8) % 4) % 4
            there_z = (z + (offset // 2) % 4) % 4
            there_core = (core + offset % 2) % 2
            to_row = (there_x // 2) * 4 + there_y
            to_col = there_z * 4 + (there_x % 2) * 2 + there_core
            src, dst, sent, got = copy(to_row * 16 + to_col)
            pltpu.make_async_remote_copy(
                src_ref=src,
                dst_ref=dst,
                send_sem=sent,
                recv_sem=got,
                device_id=(to_row, to_col),
                device_id_type=pl.DeviceIdType.MESH,
            ).start()
            return 0

        lax.fori_loop(1, parts, one, 0)

    def post(j, f):
        arrival = arrivals[f]
        at = pl.ds(pl.multiple_of(pad + me * rows + (j - f * chunks_per_field) * chunk, 8), chunk)
        to_all(
            lambda part: (
                send.at[j, pl.ds(pl.multiple_of(part * chunk, 8), chunk)],
                arrival.at[at],
                send_sem,
                recv_sems.at[f],
            )
        )
        arrival[at, :] = send[j, pl.ds(pl.multiple_of(me * chunk, 8), chunk), :]

    def group(n, f, slope_of):
        load(n).wait()
        value = slope_of(stage.at[n % slots])
        for r in range(8):
            piece = value(r)
            stacked = jnp.concatenate(
                [piece[:, q * parts : (q + 1) * parts] for q in range(width // parts)], axis=0
            )
            at = pl.ds((n % per_chunk) * 8 + r, parts, stride=chunk)
            send[n // per_chunk, at, :] = stacked.T

        @pl.when(n + slots < groups)
        def _():
            load(n + slots).start()

        if f > 0:

            @pl.when(n == f * per_field)
            def _():
                post(f * chunks_per_field - 1, f - 1)

        @pl.when((n % per_chunk == 0) & (n > f * per_field))
        def _():
            post(n // per_chunk - 1, f)

        return 0

    def plain(ref):
        return lambda r: ref[r]

    def along_x(ref):
        high, low = split(ref[...].reshape(8 * planes, width))
        slope = dot(high, high_ref[...]) + (dot(high, low_ref[...]) + dot(low, high_ref[...]))
        return lambda r: -slope[r * planes : (r + 1) * planes]

    for n in range(slots):
        load(n).start()
    for f in range(fields):
        slope_of = along_x if f == fields - 1 else plain
        lax.fori_loop(
            f * per_field,
            (f + 1) * per_field,
            lambda n, _, f=f, slope_of=slope_of: group(n, f, slope_of),
            0,
        )
    post(groups // per_chunk - 1, fields - 1)

    end = 0
    for b in range(blocks):
        end = end + sizes_ref[b]
        ends[b] = end
    windows = height // 8

    def window(g, _):
        first = 0
        for b in range(blocks - 1):
            first = first + jnp.where(ends[b] <= 8 * g, 1, 0)
        block = [first, jnp.minimum(first + 1, blocks - 1), jnp.minimum(first + 2, blocks - 1)]
        bounds[2 * g] = ends[block[0]]
        bounds[2 * g + 1] = ends[block[1]]
        skip = [jnp.clip(8 * g - ends[b] + sizes_ref[b], -8, depth - 1) + pad for b in block]

        def on_zblock(c, _):
            for k in range(3):
                place = place_ref[c, block[k]]
                source[c * 3 * windows + 3 * g + k] = (
                    skip[k] + ((place // 2) * 16 + c) * rows + (place % 2) * depth
                )
            return 0

        lax.fori_loop(0, zblocks, on_zblock, 0)
        return 0

    lax.fori_loop(0, windows, window, 0)

    slabs = col_ref.shape[1]

    def holder(i, _):
        zblock, want = i // slabs, i % slabs
        slab = 0
        for h in range(1, slabs):
            slab = jnp.where(col_ref[zblock, h] == want, h, slab)
        slab_of[i] = zblock * planes + 2 * slab
        return 0

    lax.fori_loop(0, zblocks * slabs, holder, 0)

    def arrived(f):
        block = arrivals[f].at[pl.ds(pad, (parts - 1) * rows)]
        pltpu.make_async_copy(block, block, recv_sems.at[f]).wait()

    def align(buffer, c):
        for g in range(windows):
            base = c * 3 * windows + 3 * g
            at = lax.broadcasted_iota(jnp.int32, (8, lanes), 0) + 8 * g
            one, two, three = (buffer[pl.ds(source[base + k], 8), :] for k in range(3))
            value = jnp.where(
                at < bounds[2 * g], one, jnp.where(at < bounds[2 * g + 1], two, three)
            )
            aligned[8 * g : 8 * g + 8, :] = value

    def on_z(c, _):
        align(in_z, c)
        high, low = split(aligned[...].T)
        at = pl.ds(pl.multiple_of(c * planes, planes), planes)
        for q in range(quarters):
            v_high[q, at, :] = high[q * planes : (q + 1) * planes]
            v_low[q, at, :] = low[q * planes : (q + 1) * planes]
        return 0

    def on_y(c, _):
        align(in_y, c)
        high, low = split(aligned[...])
        slope = dot(high_ref[...], high) + (dot(low_ref[...], high) + dot(high_ref[...], low))
        slope = slope.T
        at = pl.ds(pl.multiple_of(c * planes, planes), planes)
        for q in range(quarters):
            total[q, at, :] = slope[q * planes : (q + 1) * planes]
        return 0

    def on_x(c, _):
        align(in_x, c)
        slope = aligned[...].T
        at = pl.ds(pl.multiple_of(c * planes, planes), planes)
        for q in range(quarters):
            total[q, at, :] = total[q, at, :] + slope[q * planes : (q + 1) * planes]
        return 0

    for f, work in enumerate((on_z, on_y, on_x)):
        arrived(f)
        lax.fori_loop(0, zblocks, work, 0)

    block_rows = shares.shape[1] // parts
    mine = pl.ds(pl.multiple_of(me * block_rows, 8), block_rows)

    def quarter(q, _):
        value = total[q] + (
            dot(high_ref[...], v_high[q])
            + (dot(low_ref[...], v_high[q]) + dot(high_ref[...], v_low[q]))
        )
        top = jnp.max(jnp.abs(value), axis=0, keepdims=True)
        for piece in range(pieces):
            along = slice(piece * lanes, (piece + 1) * lanes)
            field[piece * height : (piece + 1) * height, :] = value[:, along]
            peaks[pl.ds(q * pieces + piece, 1), :] = top[:, along]
        for zblock in range(zblocks):
            for holding in range(slabs):
                low_row = slab_of[zblock * slabs + holding]
                target = ((zblock // 2) * slabs + holding) * block_rows + 2 * (zblock % 2)
                for piece in range(pieces):
                    at = target + 4 * piece
                    shares[q, at : at + 2, :] = field[pl.ds(low_row + piece * height, 2), :]
        to_all(
            lambda part: (
                shares.at[q, pl.ds(pl.multiple_of(part * block_rows, 8), block_rows)],
                out_ref.at[q, mine],
                share_send_sem,
                share_recv_sems,
            )
        )
        pltpu.make_async_copy(shares.at[q, mine], out_ref.at[q, mine], own_sem).start()
        return 0

    lax.fori_loop(0, quarters, quarter, 0)
    to_all(lambda part: (peaks, out_ref.at[quarters, mine], share_send_sem, share_recv_sems))
    pltpu.make_async_copy(peaks, out_ref.at[quarters, mine], own_sem).start()

    others = out_ref.at[:, pl.ds(0, (parts - 1) * block_rows)]
    own = out_ref.at[:, pl.ds(0, block_rows)]
    sent = send.at[:, pl.ds(0, (parts - 1) * chunk)]
    pltpu.make_async_copy(sent, sent, send_sem).wait()
    pltpu.make_async_copy(own, own, own_sem).wait()
    pltpu.make_async_copy(others, others, share_send_sem).wait()
    pltpu.make_async_copy(others, others, share_recv_sems).wait()


def fused(velocity, high, low, sizes, old_place, new_col, parts):
    fields, rows, planes, width = velocity.shape
    lanes = planes * width // parts
    height = width
    chunk = 24
    quarters = width // parts
    zblocks, blocks = old_place.shape
    block_rows = 16
    vmem = pl.BlockSpec(memory_space=pltpu.VMEM)
    smem = pl.BlockSpec(memory_space=pltpu.SMEM)
    anywhere = pl.BlockSpec(memory_space=pl.ANY)
    arrival = pltpu.VMEM((parts * rows + 16, lanes), jnp.float32)
    return pl.pallas_call(
        fused_kernel,
        in_specs=[anywhere, vmem, vmem, smem, smem, smem],
        out_specs=anywhere,
        out_shape=jax.ShapeDtypeStruct((quarters + 1, parts * block_rows, lanes), jnp.float32),
        scratch_shapes=[
            pltpu.VMEM((3, 8, planes, width), jnp.float32),
            pltpu.VMEM((fields * rows // chunk, parts * chunk, lanes), jnp.float32),
            arrival,
            arrival,
            arrival,
            pltpu.VMEM((height, lanes), jnp.float32),
            pltpu.VMEM((quarters, height, height), jnp.bfloat16),
            pltpu.VMEM((quarters, height, height), jnp.bfloat16),
            pltpu.VMEM((quarters, height, height), jnp.float32),
            pltpu.VMEM((height * height // lanes, lanes), jnp.float32),
            pltpu.VMEM((quarters, parts * block_rows, lanes), jnp.float32),
            pltpu.VMEM((block_rows, lanes), jnp.float32),
            pltpu.SMEM((blocks,), jnp.int32),
            pltpu.SMEM((height // 4,), jnp.int32),
            pltpu.SMEM((zblocks * 3 * height // 8,), jnp.int32),
            pltpu.SMEM((zblocks * new_col.shape[1],), jnp.int32),
            pltpu.SemaphoreType.DMA((3,)),
            pltpu.SemaphoreType.DMA,
            pltpu.SemaphoreType.DMA((3,)),
            pltpu.SemaphoreType.DMA,
            pltpu.SemaphoreType.DMA,
            pltpu.SemaphoreType.DMA,
        ],
        compiler_params=pltpu.CompilerParams(vmem_limit_bytes=63 << 20, has_side_effects=True),
        cost_estimate=pl.CostEstimate(
            flops=54 * height**3, bytes_accessed=32 << 20, transcendentals=0
        ),
        name="fused",
    )(velocity, high, low, sizes, old_place, new_col)


def finish_kernel(g_ref, p_ref, out_ref, peak_ref):
    thick, _, parts = out_ref.shape
    rows, lanes = g_ref.shape[1] // parts, g_ref.shape[2]
    chunks = rows // thick
    q = pl.program_id(0)
    for chunk in range(chunks):
        ys = slice(chunk * lanes, (chunk + 1) * lanes)
        for plane in range(thick):
            at = pl.ds(chunk * thick + plane, parts, stride=rows)
            out_ref[plane, ys, :] = g_ref[0, at, :].T
        peak_ref[ys, :] = p_ref[0, pl.ds(q * chunks + chunk, parts, stride=rows), :].T


def finish(received, parts, thick, height):
    quarters = received.shape[0] - 1
    block = (1,) + received.shape[1:]
    return pl.pallas_call(
        finish_kernel,
        grid=(quarters,),
        in_specs=[
            pl.BlockSpec(block, lambda q: (q, 0, 0)),
            pl.BlockSpec(block, lambda q: (quarters, 0, 0)),
        ],
        out_specs=[
            pl.BlockSpec((thick, height, parts), lambda q: (0, 0, q)),
            pl.BlockSpec((height, parts), lambda q: (0, q)),
        ],
        out_shape=[
            jax.ShapeDtypeStruct((thick, height, quarters * parts), jnp.float32),
            jax.ShapeDtypeStruct((height, quarters * parts), jnp.float32),
        ],
        compiler_params=pltpu.CompilerParams(vmem_limit_bytes=48 << 20),
        cost_estimate=pl.CostEstimate(flops=1 << 20, bytes_accessed=10 << 20, transcendentals=0),
        name="finish",
    )(received, received)


def on_device(velocity, y_sizes, old_place, new_col):
    fields, _, places, depth, planes, width = velocity.shape
    parts = lax.axis_size("row") * lax.axis_size("col")
    high, low = two_halves(spectral_matrix(width))
    received = fused(
        velocity.reshape(fields, places * depth, planes, width),
        high,
        low,
        y_sizes,
        old_place,
        new_col,
        parts,
    )
    field, peak = finish(received, parts, 4, width)
    return field.reshape(2, 1, 2, width, width), peak


def solution(mesh):
    in_specs = (P(None, "col", "row", None, None, None), P(), P(), P())
    out_specs = (P("row", "col", None, None, None), P())
    return jax.shard_map(
        on_device, mesh=mesh, in_specs=in_specs, out_specs=out_specs, check_vma=False
    )
```

time: 275 us -> 246 us (0.89)
  blocking collectives: 69.2 us -> 0 us
  Pallas kernels: 202 us -> 243 us
    all_to_all x1 -> x0, blocking collectives: 69.2 us -> none  [exchange(): return lax.all_to_all(blocks, BOTH, split_axis=0, concat_axis=0, tiled=True)]
    pallas_call x3 -> x2, Pallas kernels: 202 us -> 243 us  [the longest x1 239 us: fused(): pl.pallas_call(fused_kernel, in_specs=[anywhere, vmem, vmem, smem, smem,...]
where the time goes in v3:
time: 246 us
  Pallas kernels  243 us (99%)
  local copies, waits for them, and re-layouts  2.48 us (1%)
    pallas_call x1, Pallas kernels, fused(): pl.pallas_call(fused_kernel, in_specs=[anywhere, vmem, vmem, smem, smem,...  239 us

profile of v3, /device:TPU:1, one launch (start us, length us, event | category | flops | bytes accessed | tf_op | source)
XLA Modules:
  0.0 246.0 jit_solution(560706644637796586)
XLA Ops:
  0.6 239.4 %fused.1.g_ref.p_ref = f32[5,2048,128]{2,1,0:T(8,128)} custom-call(f32[3,72,32,512]{3,2,1,0:T(8,128)} %bitcast.4, bf16[512,512]{1,0:T(8,128)(2,1)} %constant.4.clone.high_ref, bf16[512,512]{1,0:T(8,128)(2,1)} %constant.5.clone.low_ref, s32[16]{0:T(128)} %sizes_ref.1, s32[16,16]{1,0:T(8,128)} %place_ref.1, s32[16,16]{1,0:T(8,128)} %col_ref.1), custom_call_target="tpu_custom_call" | custom-call | flops 7247757312 | bytes 33554432 | tf_op jit(solution)/shard_map/fused/pallas_call | solution.py:291
  240.0 0.0 copy-start
  240.0 2.5 %copy-done = f32[5,2048,128]{2,1,0:T(8,128)S(1)} copy-done((f32[5,2048,128]{2,1,0:T(8,128)S(1)}, f32[5,2048,128]{2,1,0:T(8,128)}, u32[]{:S(2)}) %copy-start) | copy-done | bytes 5242904
  242.5 3.5 %finish.1 = (f32[4,512,512]{2,1,0:T(8,128)}, f32[512,512]{1,0:T(8,128)}) custom-call(f32[5,2048,128]{2,1,0:T(8,128)S(1)} %copy-done, f32[5,2048,128]{2,1,0:T(8,128)S(1)} %copy-done), custom_call_target="tpu_custom_call" | custom-call | flops 1048576 | bytes 10485760 | tf_op jit(solution)/shard_map/finish/pallas_call | solution.py:344
Async XLA Ops:
  240.0 2.5 %copy-start = (f32[5,2048,128]{2,1,0:T(8,128)S(1)}, f32[5,2048,128]{2,1,0:T(8,128)}, u32[]{:S(2)}) copy-start(f32[5,2048,128]{2,1,0:T(8,128)} %fused.1.g_ref.p_ref) | copy-start | bytes 15728644

commit v4 on v3

v4 whole, which is shorter than its diff:
```python
import math

import jax
import jax.numpy as jnp
import numpy as np
from jax import lax
from jax.experimental import pallas as pl
from jax.experimental.pallas import tpu as pltpu
from jax.sharding import PartitionSpec as P


def spectral_matrix(count):
    gap = (np.arange(count)[:, None] - np.arange(count)[None, :]) % count
    angle = gap.astype(np.float64) * (math.pi / count)
    parity = 1.0 - 2.0 * (gap % 2)
    divisor = np.where(gap == 0, 1.0, np.sin(angle))
    return np.where(gap == 0, 0.0, parity * np.cos(angle) / divisor * (2.0 / count))


def two_halves(matrix):
    high = matrix.astype(np.float32).astype(jnp.bfloat16)
    low = (matrix - high.astype(np.float64)).astype(np.float32).astype(jnp.bfloat16)
    return jnp.asarray(high), jnp.asarray(low)


def split(value):
    high = value.astype(jnp.bfloat16)
    return high, (value - high.astype(jnp.float32)).astype(jnp.bfloat16)


def dot(a, b):
    return jnp.dot(a, b, preferred_element_type=jnp.float32)


def fused_kernel(
    v_ref, high_ref, low_ref, sizes_ref, place_ref, col_ref, out_ref,
    stage, send, in_x, in_a, in_b, aligned, z_high, z_low, y_high, y_low, total, field, shares,
    ends, bounds, source, slab_of,
    in_sems, send_sem, recv_sems, share_send_sems, share_recv_sems, own_sem,
):
    fields, rows, planes, width = v_ref.shape
    lanes = send.shape[2]
    parts = lanes
    chunk = send.shape[1] // parts
    per_field = rows // 8
    groups = fields * per_field
    per_chunk = chunk // 8
    chunks_per_field = rows // chunk
    slots = stage.shape[0]
    quarters = total.shape[0]
    half = quarters // 2
    height = total.shape[2]
    pieces = height // lanes
    zblocks, blocks = place_ref.shape
    slabs = col_ref.shape[1]
    depth = rows // 2
    pad = (in_x.shape[0] - parts * rows) // 2
    arrivals = (in_x, in_a, in_b)
    row, col = lax.axis_index("row"), lax.axis_index("col")
    me = row * 16 + col
    x, y, z, core = (row // 4) * 2 + (col // 2) % 2, row % 4, col // 4, col % 2

    def partner(i):
        offset = ((i + core * (parts - 2 * i)) * 37) % parts
        there_x = (x + offset // 32) % 4
        there_y = (y + (offset // 8) % 4) % 4
        there_z = (z + (offset // 2) % 4) % 4
        there_core = (core + offset % 2) % 2
        return (there_x // 2) * 4 + there_y, there_z * 4 + (there_x % 2) * 2 + there_core

    barrier = pltpu.get_barrier_semaphore()

    def greet(i, _):
        pl.semaphore_signal(
            barrier, inc=1, device_id=partner(i), device_id_type=pl.DeviceIdType.MESH
        )
        return 0

    def loads(f, n):
        at = pl.ds((n - f * per_field) * 8, 8)
        slot = n % slots
        if f == 0:
            return [pltpu.make_async_copy(v_ref.at[0, at], stage.at[slot], in_sems.at[slot, 0])]
        wide = width // 2
        xs = pl.ds((f - 1) * wide, wide)
        return [
            pltpu.make_async_copy(
                v_ref.at[2 - k, at, :, xs],
                stage.at[slot, :, :, pl.ds(k * wide, wide)],
                in_sems.at[slot, k],
            )
            for k in range(2)
        ]

    def start_load(f, n):
        for copy in loads(f, n):
            copy.start()

    def to_all(copy):
        def one(i, _):
            to_row, to_col = partner(i)
            src, dst, sent, got = copy(to_row * 16 + to_col)
            pltpu.make_async_remote_copy(
                src_ref=src,
                dst_ref=dst,
                send_sem=sent,
                recv_sem=got,
                device_id=(to_row, to_col),
                device_id_type=pl.DeviceIdType.MESH,
            ).start()
            return 0

        lax.fori_loop(1, parts, one, 0)

    def post(j, f):
        arrival = arrivals[f]
        at = pl.ds(pl.multiple_of(pad + me * rows + (j - f * chunks_per_field) * chunk, 8), chunk)
        to_all(
            lambda part: (
                send.at[j, pl.ds(pl.multiple_of(part * chunk, 8), chunk)],
                arrival.at[at],
                send_sem,
                recv_sems.at[f],
            )
        )
        arrival[at, :] = send[j, pl.ds(pl.multiple_of(me * chunk, 8), chunk), :]

    def group(n, f, slope_of):
        for copy in loads(f, n):
            copy.wait()
        value = slope_of(stage.at[n % slots])
        for r in range(8):
            piece = value(r)
            stacked = jnp.concatenate(
                [piece[:, q * parts : (q + 1) * parts] for q in range(width // parts)], axis=0
            )
            at = pl.ds((n % per_chunk) * 8 + r, parts, stride=chunk)
            send[n // per_chunk, at, :] = stacked.T

        later = n + slots
        for g in range(f, min(f + 2, fields)):

            @pl.when((later >= g * per_field) & (later < (g + 1) * per_field))
            def _(g=g):
                start_load(g, later)

        if f > 0:

            @pl.when(n == f * per_field)
            def _():
                post(f * chunks_per_field - 1, f - 1)

        @pl.when((n % per_chunk == 0) & (n > f * per_field))
        def _():
            post(n // per_chunk - 1, f)

        return 0

    def plain(ref):
        return lambda r: ref[r]

    def along_x(ref):
        high, low = split(ref[...].reshape(8 * planes, width))
        slope = dot(high, high_ref[...]) + (dot(high, low_ref[...]) + dot(low, high_ref[...]))
        return lambda r: -slope[r * planes : (r + 1) * planes]

    lax.fori_loop(1, parts, greet, 0)
    for n in range(slots):
        start_load(0, n)
    pl.semaphore_wait(barrier, parts - 1)
    for f in range(fields):
        slope_of = plain if f else along_x
        lax.fori_loop(
            f * per_field,
            (f + 1) * per_field,
            lambda n, _, f=f, slope_of=slope_of: group(n, f, slope_of),
            0,
        )
    post(groups // per_chunk - 1, fields - 1)

    end = 0
    for b in range(blocks):
        end = end + sizes_ref[b]
        ends[b] = end
    windows = height // 8

    def window(g, _):
        first = 0
        for b in range(blocks - 1):
            first = first + jnp.where(ends[b] <= 8 * g, 1, 0)
        block = [first, jnp.minimum(first + 1, blocks - 1), jnp.minimum(first + 2, blocks - 1)]
        bounds[2 * g] = ends[block[0]]
        bounds[2 * g + 1] = ends[block[1]]
        skip = [jnp.clip(8 * g - ends[b] + sizes_ref[b], -8, depth - 1) + pad for b in block]

        def on_zblock(c, _):
            for k in range(3):
                place = place_ref[c, block[k]]
                source[c * 3 * windows + 3 * g + k] = (
                    skip[k] + ((place >> 1) * 16 + c) * rows + (place & 1) * depth
                )
            return 0

        lax.fori_loop(0, zblocks, on_zblock, 0)
        return 0

    lax.fori_loop(0, windows, window, 0)

    def holder(i, _):
        zblock, want = i // slabs, i % slabs
        slab = 0
        for h in range(1, slabs):
            slab = jnp.where(col_ref[zblock, h] == want, h, slab)
        slab_of[i] = zblock * planes + 2 * slab
        return 0

    lax.fori_loop(0, zblocks * slabs, holder, 0)

    def arrived(f):
        block = arrivals[f].at[pl.ds(pad, (parts - 1) * rows)]
        pltpu.make_async_copy(block, block, recv_sems.at[f]).wait()

    def align(buffer, c):
        for g in range(windows):
            base = c * 3 * windows + 3 * g
            at = lax.broadcasted_iota(jnp.int32, (8, lanes), 0) + 8 * g
            one, two, three = (buffer[pl.ds(source[base + k], 8), :] for k in range(3))
            value = jnp.where(
                at < bounds[2 * g], one, jnp.where(at < bounds[2 * g + 1], two, three)
            )
            aligned[8 * g : 8 * g + 8, :] = value

    def on_x(c, _):
        align(in_x, c)
        slope = aligned[...].T
        at = pl.ds(pl.multiple_of(c * planes, planes), planes)
        for q in range(quarters):
            total[q, at, :] = slope[q * planes : (q + 1) * planes]
        return 0

    def on_half(h, c):
        align(arrivals[1 + h], c)
        high, low = split(aligned[...].T)
        at = pl.ds(pl.multiple_of(c * planes, planes), planes)
        for q in range(half):
            zs = slice(q * planes, (q + 1) * planes)
            ys = slice((half + q) * planes, (half + q + 1) * planes)
            z_high[half * h + q, at, :] = high[zs]
            z_low[half * h + q, at, :] = low[zs]
            y_high[half * h + q, at, :] = high[ys]
            y_low[half * h + q, at, :] = low[ys]
        return 0

    block_rows = shares.shape[1] // parts
    mine = pl.ds(pl.multiple_of(me * block_rows, 8), block_rows)

    def quarter(h, k):
        q = half * h + k
        along_z = dot(high_ref[...], z_high[q]) + (
            dot(low_ref[...], z_high[q]) + dot(high_ref[...], z_low[q])
        )
        along_y = dot(y_high[q], high_ref[...]) + (
            dot(y_high[q], low_ref[...]) + dot(y_low[q], high_ref[...])
        )
        value = total[q] + (along_z - along_y)
        top = jnp.max(jnp.abs(value), axis=0, keepdims=True)
        for piece in range(pieces):
            along = slice(piece * lanes, (piece + 1) * lanes)
            field[piece * height : (piece + 1) * height, :] = value[:, along]
            aligned[pl.ds(k * pieces + piece, 1), :] = top[:, along]
        first = pl.multiple_of(k * 4 * pieces, 8)
        for zblock in range(zblocks):
            for holding in range(slabs):
                low_row = slab_of[zblock * slabs + holding]
                target = ((zblock // 2) * slabs + holding) * block_rows + 2 * (zblock % 2)
                for piece in range(pieces):
                    shares[h, pl.ds(first + target + 4 * piece, 2), :] = field[
                        pl.ds(low_row + piece * height, 2), :
                    ]
        return 0

    arrived(0)
    lax.fori_loop(0, zblocks, on_x, 0)
    for h in range(2):
        arrived(1 + h)
        lax.fori_loop(0, zblocks, lambda c, _, h=h: on_half(h, c), 0)
        lax.fori_loop(0, half, lambda k, _, h=h: quarter(h, k), 0)
        tops = aligned[: half * pieces, :]

        def top_rows(part, _, h=h, tops=tops):
            at = pl.multiple_of(part * block_rows + half * 4 * pieces, 8)
            shares[h, pl.ds(at, half * pieces), :] = tops
            return 0

        lax.fori_loop(0, parts, top_rows, 0)
        to_all(
            lambda part, h=h: (
                shares.at[h, pl.ds(pl.multiple_of(part * block_rows, 8), block_rows)],
                out_ref.at[h, mine],
                share_send_sems.at[h],
                share_recv_sems.at[h],
            )
        )
        pltpu.make_async_copy(shares.at[h, mine], out_ref.at[h, mine], own_sem.at[h]).start()

    sent = send.at[:, pl.ds(0, (parts - 1) * chunk)]
    pltpu.make_async_copy(sent, sent, send_sem).wait()
    for h in range(2):
        others = out_ref.at[h, pl.ds(0, (parts - 1) * block_rows)]
        own = out_ref.at[h, pl.ds(0, block_rows)]
        pltpu.make_async_copy(own, own, own_sem.at[h]).wait()
        pltpu.make_async_copy(others, others, share_send_sems.at[h]).wait()
        pltpu.make_async_copy(others, others, share_recv_sems.at[h]).wait()


def fused(velocity, high, low, sizes, old_place, new_col, parts):
    fields, rows, planes, width = velocity.shape
    lanes = planes * width // parts
    height = width
    chunk = 24
    quarters = width // parts
    zblocks, blocks = old_place.shape
    block_rows = 40
    vmem = pl.BlockSpec(memory_space=pltpu.VMEM)
    smem = pl.BlockSpec(memory_space=pltpu.SMEM)
    anywhere = pl.BlockSpec(memory_space=pl.ANY)
    arrival = pltpu.VMEM((parts * rows + 16, lanes), jnp.float32)
    operand = pltpu.VMEM((quarters, height, height), jnp.bfloat16)
    return pl.pallas_call(
        fused_kernel,
        in_specs=[anywhere, vmem, vmem, smem, smem, smem],
        out_specs=anywhere,
        out_shape=jax.ShapeDtypeStruct((2, parts * block_rows, lanes), jnp.float32),
        scratch_shapes=[
            pltpu.VMEM((3, 8, planes, width), jnp.float32),
            pltpu.VMEM((fields * rows // chunk, parts * chunk, lanes), jnp.float32),
            arrival,
            arrival,
            arrival,
            pltpu.VMEM((height, lanes), jnp.float32),
            operand,
            operand,
            operand,
            operand,
            pltpu.VMEM((quarters, height, height), jnp.float32),
            pltpu.VMEM((height * height // lanes, lanes), jnp.float32),
            pltpu.VMEM((2, parts * block_rows, lanes), jnp.float32),
            pltpu.SMEM((blocks,), jnp.int32),
            pltpu.SMEM((height // 4,), jnp.int32),
            pltpu.SMEM((zblocks * 3 * height // 8,), jnp.int32),
            pltpu.SMEM((zblocks * new_col.shape[1],), jnp.int32),
            pltpu.SemaphoreType.DMA((3, 2)),
            pltpu.SemaphoreType.DMA,
            pltpu.SemaphoreType.DMA((3,)),
            pltpu.SemaphoreType.DMA((2,)),
            pltpu.SemaphoreType.DMA((2,)),
            pltpu.SemaphoreType.DMA((2,)),
        ],
        compiler_params=pltpu.CompilerParams(
            vmem_limit_bytes=63 << 20, has_side_effects=True, collective_id=0
        ),
        cost_estimate=pl.CostEstimate(
            flops=54 * height**3, bytes_accessed=32 << 20, transcendentals=0
        ),
        name="fused",
    )(velocity, high, low, sizes, old_place, new_col)


def finish_kernel(g_ref, out_ref, peak_ref):
    thick, height, parts = out_ref.shape
    rows, lanes = g_ref.shape[1] // parts, g_ref.shape[2]
    chunks = height // lanes
    k = pl.program_id(0) % 2
    for chunk in range(chunks):
        ys = slice(chunk * lanes, (chunk + 1) * lanes)
        for plane in range(thick):
            at = pl.ds((k * chunks + chunk) * thick + plane, parts, stride=rows)
            out_ref[plane, ys, :] = g_ref[0, at, :].T
        tops = pl.ds(2 * chunks * thick + k * chunks + chunk, parts, stride=rows)
        peak_ref[ys, :] = g_ref[0, tops, :].T


def finish(received, parts, thick, height):
    quarters = height // parts
    return pl.pallas_call(
        finish_kernel,
        grid=(quarters,),
        in_specs=[pl.BlockSpec((1,) + received.shape[1:], lambda q: (q // 2, 0, 0))],
        out_specs=[
            pl.BlockSpec((thick, height, parts), lambda q: (0, 0, q)),
            pl.BlockSpec((height, parts), lambda q: (0, q)),
        ],
        out_shape=[
            jax.ShapeDtypeStruct((thick, height, quarters * parts), jnp.float32),
            jax.ShapeDtypeStruct((height, quarters * parts), jnp.float32),
        ],
        compiler_params=pltpu.CompilerParams(vmem_limit_bytes=63 << 20),
        cost_estimate=pl.CostEstimate(flops=1 << 20, bytes_accessed=10 << 20, transcendentals=0),
        name="finish",
    )(received)


def on_device(velocity, y_sizes, old_place, new_col):
    fields, _, places, depth, planes, width = velocity.shape
    parts = lax.axis_size("row") * lax.axis_size("col")
    high, low = two_halves(spectral_matrix(width))
    received = fused(
        velocity.reshape(fields, places * depth, planes, width),
        high,
        low,
        y_sizes,
        old_place,
        new_col,
        parts,
    )
    field, peak = finish(received, parts, 4, width)
    return field.reshape(2, 1, 2, width, width), peak


def solution(mesh):
    in_specs = (P(None, "col", "row", None, None, None), P(), P(), P())
    out_specs = (P("row", "col", None, None, None), P())
    return jax.shard_map(
        on_device, mesh=mesh, in_specs=in_specs, out_specs=out_specs, check_vma=False
    )
```

time: 246 us -> 239 us (0.972)
  Pallas kernels: 243 us -> 238 us
  local copies, waits for them, and re-layouts: 2.48 us -> 0 us
    pallas_call x1, Pallas kernels: 239 us -> 232 us  [fused(): pl.pallas_call(fused_kernel, in_specs=[anywhere, vmem, vmem, smem, smem,...]
    pallas_call x1, Pallas kernels: 3.51 us -> 6.77 us  [finish(): pl.pallas_call(finish_kernel, grid=(quarters,), in_specs=[pl.BlockSpec((1...]
    unnamed x2 -> x0, local copies, waits for them, and re-layouts: 2.48 us -> none
where the time goes in v4:
time: 239 us
  Pallas kernels  238 us (100%)
    pallas_call x1, Pallas kernels, fused(): pl.pallas_call(fused_kernel, in_specs=[anywhere, vmem, vmem, smem, smem,...  232 us
    pallas_call x1, Pallas kernels, finish(): pl.pallas_call(finish_kernel, grid=(quarters,), in_specs=[pl.BlockSpec((1...  6.77 us

profile of v4, /device:TPU:1, one launch (start us, length us, event | category | flops | bytes accessed | tf_op | source)
XLA Modules:
  0.0 239.0 jit_solution(1130059217976701685)
XLA Ops:
  0.6 231.5 %fused.1.g_ref = f32[2,5120,128]{2,1,0:T(8,128)} custom-call(f32[3,72,32,512]{3,2,1,0:T(8,128)} %bitcast.4, bf16[512,512]{1,0:T(8,128)(2,1)} %constant.4.clone.high_ref, bf16[512,512]{1,0:T(8,128)(2,1)} %constant.5.clone.low_ref, s32[16]{0:T(128)} %sizes_ref.1, s32[16,16]{1,0:T(8,128)} %place_ref.1, s32[16,16]{1,0:T(8,128)} %col_ref.1), custom_call_target="tpu_custom_call" | custom-call | flops 7247757312 | bytes 33554432 | tf_op jit(solution)/shard_map/fused/pallas_call | solution.py:329
  232.2 6.8 %finish.1 = (f32[4,512,512]{2,1,0:T(8,128)}, f32[512,512]{1,0:T(8,128)}) custom-call(f32[2,5120,128]{2,1,0:T(8,128)} %fused.1.g_ref), custom_call_target="tpu_custom_call" | custom-call | flops 1048576 | bytes 10485760 | tf_op jit(solution)/shard_map/finish/pallas_call | solution.py:385

commit v5 on v4

--- a/solution.py
+++ b/solution.py
@@ -33,10 +33,12 @@
 
 
 def fused_kernel(
-    v_ref, high_ref, low_ref, sizes_ref, place_ref, col_ref, out_ref,
-    stage, send, in_x, in_a, in_b, aligned, z_high, z_low, y_high, y_low, total, field, shares,
+    v_ref, high_ref, low_ref, sizes_ref, place_ref, col_ref, out_ref, peak_ref,
+    stage, send, in_a, in_x, in_b, aligned, z_high, z_low, y_high, y_low, total, field, shares,
+    tops,
     ends, bounds, source, slab_of,
     in_sems, send_sem, recv_sems, share_send_sems, share_recv_sems, own_sem,
+    peak_send_sems, peak_recv_sems, peak_own_sems, pair_send_sems, pair_recv_sems,
 ):
     fields, rows, planes, width = v_ref.shape
     lanes = send.shape[2]
@@ -55,34 +57,45 @@
     slabs = col_ref.shape[1]
     depth = rows // 2
     pad = (in_x.shape[0] - parts * rows) // 2
-    arrivals = (in_x, in_a, in_b)
+    arrivals = (in_a, in_x, in_b)
+    x_section = 1
     row, col = lax.axis_index("row"), lax.axis_index("col")
     me = row * 16 + col
-    x, y, z, core = (row // 4) * 2 + (col // 2) % 2, row % 4, col // 4, col % 2
+    div, rem = lax.div, lax.rem
+    chip, core = row * 8 + div(col, 2), rem(col, 2)
+    x, y = div(row, 4) * 2 + rem(div(col, 2), 2), rem(row, 4)
+    z = div(col, 4)
+
+    def chip_at(offset):
+        there_x = rem(x + div(offset, 16), 4)
+        there_y = rem(y + div(offset, 4), 4)
+        there_z = rem(z + offset, 4)
+        return div(there_x, 2) * 4 + there_y, there_z * 4 + rem(there_x, 2) * 2
 
     def partner(i):
-        offset = ((i + core * (parts - 2 * i)) * 37) % parts
-        there_x = (x + offset // 32) % 4
-        there_y = (y + (offset // 8) % 4) % 4
-        there_z = (z + (offset // 2) % 4) % 4
-        there_core = (core + offset % 2) % 2
-        return (there_x // 2) * 4 + there_y, there_z * 4 + (there_x % 2) * 2 + there_core
+        offset = rem((i + core * (parts - 2 * i)) * 37, parts)
+        to_row, first = chip_at(div(offset, 2))
+        return to_row, first + rem(core + offset, 2)
 
     barrier = pltpu.get_barrier_semaphore()
 
     def greet(i, _):
+        other = rem(me + i, parts)
         pl.semaphore_signal(
-            barrier, inc=1, device_id=partner(i), device_id_type=pl.DeviceIdType.MESH
+            barrier,
+            inc=1,
+            device_id=(div(other, 16), rem(other, 16)),
+            device_id_type=pl.DeviceIdType.MESH,
         )
         return 0
 
     def loads(f, n):
         at = pl.ds((n - f * per_field) * 8, 8)
         slot = n % slots
-        if f == 0:
+        if f == x_section:
             return [pltpu.make_async_copy(v_ref.at[0, at], stage.at[slot], in_sems.at[slot, 0])]
         wide = width // 2
-        xs = pl.ds((f - 1) * wide, wide)
+        xs = pl.ds((f // 2) * wide, wide)
         return [
             pltpu.make_async_copy(
                 v_ref.at[2 - k, at, :, xs],
@@ -169,7 +182,7 @@
         start_load(0, n)
     pl.semaphore_wait(barrier, parts - 1)
     for f in range(fields):
-        slope_of = plain if f else along_x
+        slope_of = along_x if f == x_section else plain
         lax.fori_loop(
             f * per_field,
             (f + 1) * per_field,
@@ -239,7 +252,7 @@
         return 0
 
     def on_half(h, c):
-        align(arrivals[1 + h], c)
+        align(arrivals[2 * h], c)
         high, low = split(aligned[...].T)
         at = pl.ds(pl.multiple_of(c * planes, planes), planes)
         for q in range(half):
@@ -267,7 +280,7 @@
         for piece in range(pieces):
             along = slice(piece * lanes, (piece + 1) * lanes)
             field[piece * height : (piece + 1) * height, :] = value[:, along]
-            aligned[pl.ds(k * pieces + piece, 1), :] = top[:, along]
+            tops[h, pl.ds(k * pieces + piece, 1), :] = top[:, along]
         first = pl.multiple_of(k * 4 * pieces, 8)
         for zblock in range(zblocks):
             for holding in range(slabs):
@@ -279,20 +292,43 @@
                     ]
         return 0
 
-    arrived(0)
-    lax.fori_loop(0, zblocks, on_x, 0)
+    def give_peaks(h):
+        mine = peak_ref.at[h, chip, core]
+
+        def one(i, _):
+            to_row, first = chip_at(rem(i * 37, parts // 2))
+            pltpu.make_async_remote_copy(
+                src_ref=tops.at[h],
+                dst_ref=mine,
+                send_sem=peak_send_sems.at[h],
+                recv_sem=peak_recv_sems.at[h],
+                device_id=(to_row, first + core),
+                device_id_type=pl.DeviceIdType.MESH,
+            ).start()
+            return 0
+
+        lax.fori_loop(1, parts // 2, one, 0)
+        pltpu.make_async_copy(tops.at[h], mine, peak_own_sems.at[h]).start()
+
+    def pair_copy(h):
+        held = peak_ref.at[h, :, core]
+        return pltpu.make_async_remote_copy(
+            src_ref=held,
+            dst_ref=held,
+            send_sem=pair_send_sems.at[h],
+            recv_sem=pair_recv_sems.at[h],
+            device_id=(row, col + 1 - 2 * core),
+            device_id_type=pl.DeviceIdType.MESH,
+        )
+
     for h in range(2):
-        arrived(1 + h)
+        arrived(2 * h)
         lax.fori_loop(0, zblocks, lambda c, _, h=h: on_half(h, c), 0)
+        if h == 0:
+            arrived(x_section)
+            lax.fori_loop(0, zblocks, on_x, 0)
         lax.fori_loop(0, half, lambda k, _, h=h: quarter(h, k), 0)
-        tops = aligned[: half * pieces, :]
-
-        def top_rows(part, _, h=h, tops=tops):
-            at = pl.multiple_of(part * block_rows + half * 4 * pieces, 8)
-            shares[h, pl.ds(at, half * pieces), :] = tops
-            return 0
-
-        lax.fori_loop(0, parts, top_rows, 0)
+        give_peaks(h)
         to_all(
             lambda part, h=h: (
                 shares.at[h, pl.ds(pl.multiple_of(part * block_rows, 8), block_rows)],
@@ -303,9 +339,16 @@
         )
         pltpu.make_async_copy(shares.at[h, mine], out_ref.at[h, mine], own_sem.at[h]).start()
 
+    for h in range(2):
+        others = peak_ref.at[h, pl.ds(0, parts // 2 - 1), 0]
+        pltpu.make_async_copy(tops.at[h], peak_ref.at[h, chip, core], peak_own_sems.at[h]).wait()
+        pltpu.make_async_copy(others, others, peak_send_sems.at[h]).wait()
+        pltpu.make_async_copy(others, others, peak_recv_sems.at[h]).wait()
+        pair_copy(h).start()
     sent = send.at[:, pl.ds(0, (parts - 1) * chunk)]
     pltpu.make_async_copy(sent, sent, send_sem).wait()
     for h in range(2):
+        pair_copy(h).wait()
         others = out_ref.at[h, pl.ds(0, (parts - 1) * block_rows)]
         own = out_ref.at[h, pl.ds(0, block_rows)]
         pltpu.make_async_copy(own, own, own_sem.at[h]).wait()
@@ -320,7 +363,7 @@
     chunk = 24
     quarters = width // parts
     zblocks, blocks = old_place.shape
-    block_rows = 40
+    block_rows = 32
     vmem = pl.BlockSpec(memory_space=pltpu.VMEM)
     smem = pl.BlockSpec(memory_space=pltpu.SMEM)
     anywhere = pl.BlockSpec(memory_space=pl.ANY)
@@ -329,8 +372,11 @@
     return pl.pallas_call(
         fused_kernel,
         in_specs=[anywhere, vmem, vmem, smem, smem, smem],
-        out_specs=anywhere,
-        out_shape=jax.ShapeDtypeStruct((2, parts * block_rows, lanes), jnp.float32),
+        out_specs=[anywhere, anywhere],
+        out_shape=[
+            jax.ShapeDtypeStruct((2, parts * block_rows, lanes), jnp.float32),
+            jax.ShapeDtypeStruct((2, parts // 2, 2, 8, lanes), jnp.float32),
+        ],
         scratch_shapes=[
             pltpu.VMEM((3, 8, planes, width), jnp.float32),
             pltpu.VMEM((fields * rows // chunk, parts * chunk, lanes), jnp.float32),
@@ -345,6 +391,7 @@
             pltpu.VMEM((quarters, height, height), jnp.float32),
             pltpu.VMEM((height * height // lanes, lanes), jnp.float32),
             pltpu.VMEM((2, parts * block_rows, lanes), jnp.float32),
+            pltpu.VMEM((2, 8, lanes), jnp.float32),
             pltpu.SMEM((blocks,), jnp.int32),
             pltpu.SMEM((height // 4,), jnp.int32),
             pltpu.SMEM((zblocks * 3 * height // 8,), jnp.int32),
@@ -352,10 +399,8 @@
             pltpu.SemaphoreType.DMA((3, 2)),
             pltpu.SemaphoreType.DMA,
             pltpu.SemaphoreType.DMA((3,)),
-            pltpu.SemaphoreType.DMA((2,)),
-            pltpu.SemaphoreType.DMA((2,)),
-            pltpu.SemaphoreType.DMA((2,)),
-        ],
+        ]
+        + [pltpu.SemaphoreType.DMA((2,))] * 8,
         compiler_params=pltpu.CompilerParams(
             vmem_limit_bytes=63 << 20, has_side_effects=True, collective_id=0
         ),
@@ -366,7 +411,7 @@
     )(velocity, high, low, sizes, old_place, new_col)
 
 
-def finish_kernel(g_ref, out_ref, peak_ref):
+def finish_kernel(g_ref, p_ref, out_ref, peak_ref):
     thick, height, parts = out_ref.shape
     rows, lanes = g_ref.shape[1] // parts, g_ref.shape[2]
     chunks = height // lanes
@@ -376,16 +421,19 @@
         for plane in range(thick):
             at = pl.ds((k * chunks + chunk) * thick + plane, parts, stride=rows)
             out_ref[plane, ys, :] = g_ref[0, at, :].T
-        tops = pl.ds(2 * chunks * thick + k * chunks + chunk, parts, stride=rows)
-        peak_ref[ys, :] = g_ref[0, tops, :].T
-
-
-def finish(received, parts, thick, height):
+        tops = pl.ds(k * chunks + chunk, parts, stride=2 * chunks)
+        peak_ref[ys, :] = p_ref[0, tops, :].T
+
+
+def finish(received, tops, parts, thick, height):
     quarters = height // parts
     return pl.pallas_call(
         finish_kernel,
         grid=(quarters,),
-        in_specs=[pl.BlockSpec((1,) + received.shape[1:], lambda q: (q // 2, 0, 0))],
+        in_specs=[
+            pl.BlockSpec((1,) + received.shape[1:], lambda q: (q // 2, 0, 0)),
+            pl.BlockSpec((1,) + tops.shape[1:], lambda q: (q // 2, 0, 0)),
+        ],
         out_specs=[
             pl.BlockSpec((thick, height, parts), lambda q: (0, 0, q)),
             pl.BlockSpec((height, parts), lambda q: (0, q)),
@@ -394,17 +442,17 @@
             jax.ShapeDtypeStruct((thick, height, quarters * parts), jnp.float32),
             jax.ShapeDtypeStruct((height, quarters * parts), jnp.float32),
         ],
-        compiler_params=pltpu.CompilerParams(vmem_limit_bytes=63 << 20),
+        compiler_params=pltpu.CompilerParams(vmem_limit_bytes=32 << 20),
         cost_estimate=pl.CostEstimate(flops=1 << 20, bytes_accessed=10 << 20, transcendentals=0),
         name="finish",
-    )(received)
+    )(received, tops)
 
 
 def on_device(velocity, y_sizes, old_place, new_col):
     fields, _, places, depth, planes, width = velocity.shape
     parts = lax.axis_size("row") * lax.axis_size("col")
     high, low = two_halves(spectral_matrix(width))
-    received = fused(
+    received, tops = fused(
         velocity.reshape(fields, places * depth, planes, width),
         high,
         low,
@@ -413,7 +461,8 @@
         new_col,
         parts,
     )
-    field, peak = finish(received, parts, 4, width)
+    tops = tops.reshape(2, parts * 8, parts)
+    field, peak = finish(received, tops, parts, 4, width)
     return field.reshape(2, 1, 2, width, width), peak
 
 

time: 239 us -> 228 us (0.954)
  Pallas kernels: 238 us -> 224 us
  local copies, waits for them, and re-layouts: 0 us -> 3.41 us
    pallas_call x1, Pallas kernels: 232 us -> 219 us  [fused(): pl.pallas_call(fused_kernel, in_specs=[anywhere, vmem, vmem, smem, smem,...]
    unnamed x0 -> x4, local copies, waits for them, and re-layouts: none -> 3.41 us
where the time goes in v5:
time: 228 us
  Pallas kernels  224 us (98%)
  local copies, waits for them, and re-layouts  3.41 us (1%)
    pallas_call x1, Pallas kernels, fused(): pl.pallas_call(fused_kernel, in_specs=[anywhere, vmem, vmem, smem, smem,...  219 us

profile of v5, /device:TPU:1, one launch (start us, length us, event | category | flops | bytes accessed | tf_op | source)
XLA Modules:
  0.0 227.7 jit_solution(7160731321401223728)
XLA Ops:
  0.6 219.3 %fused.1 = (f32[2,4096,128]{2,1,0:T(8,128)}, f32[2,64,2,8,128]{4,3,2,1,0:T(8,128)}) custom-call(f32[3,72,32,512]{3,2,1,0:T(8,128)} %bitcast.6, bf16[512,512]{1,0:T(8,128)(2,1)} %constant.4.clone.high_ref, bf16[512,512]{1,0:T(8,128)(2,1)} %constant.5.clone.low_ref, s32[16]{0:T(128)} %sizes_ref.1, s32[16,16]{1,0:T(8,128)} %place_ref.1, s32[16,16]{1,0:T(8,128)} %col_ref.1), custom_call_target="tpu_custom_call" | custom-call | flops 7247757312 | bytes 33554432 | tf_op jit(solution)/shard_map/fused/pallas_call | solution.py:372
  219.9 0.0 copy-start
  219.9 2.2 copy-done
  222.1 0.0 copy-start.1
  222.1 1.2 copy-done.1
  223.3 4.4 %finish.1 = (f32[4,512,512]{2,1,0:T(8,128)}, f32[512,512]{1,0:T(8,128)}) custom-call(f32[2,4096,128]{2,1,0:T(8,128)S(1)} %copy-done, f32[2,1024,128]{2,1,0:T(8,128)S(1)} %bitcast.5), custom_call_target="tpu_custom_call" | custom-call | flops 1048576 | bytes 10485760 | tf_op jit(solution)/shard_map/finish/pallas_call | solution.py:430
Async XLA Ops:
  219.9 2.2 copy-start
  222.1 1.2 copy-start.1

commit v6 on v5

--- a/solution.py
+++ b/solution.py
@@ -35,10 +35,10 @@
 def fused_kernel(
     v_ref, high_ref, low_ref, sizes_ref, place_ref, col_ref, out_ref, peak_ref,
     stage, send, in_a, in_x, in_b, aligned, z_high, z_low, y_high, y_low, total, field, shares,
-    tops,
+    tops, got, got_tops, ready, ready_tops,
     ends, bounds, source, slab_of,
-    in_sems, send_sem, recv_sems, share_send_sems, share_recv_sems, own_sem,
-    peak_send_sems, peak_recv_sems, peak_own_sems, pair_send_sems, pair_recv_sems,
+    in_sems, send_sem, recv_sems, share_send_sems, share_recv_sems,
+    peak_send_sems, peak_recv_sems, pair_send_sems, pair_recv_sems, out_sems, out_tops_sem,
 ):
     fields, rows, planes, width = v_ref.shape
     lanes = send.shape[2]
@@ -138,7 +138,7 @@
         )
         arrival[at, :] = send[j, pl.ds(pl.multiple_of(me * chunk, 8), chunk), :]
 
-    def group(n, f, slope_of):
+    def group(n, f, slope_of, sending=True):
         for copy in loads(f, n):
             copy.wait()
         value = slope_of(stage.at[n % slots])
@@ -157,13 +157,16 @@
             def _(g=g):
                 start_load(g, later)
 
+        if not sending:
+            return 0
+
         if f > 0:
 
             @pl.when(n == f * per_field)
             def _():
                 post(f * chunks_per_field - 1, f - 1)
 
-        @pl.when((n % per_chunk == 0) & (n > f * per_field))
+        @pl.when((n % per_chunk == 0) & (n > (f * per_field if f else per_chunk)))
         def _():
             post(n // per_chunk - 1, f)
 
@@ -180,11 +183,13 @@
     lax.fori_loop(1, parts, greet, 0)
     for n in range(slots):
         start_load(0, n)
+    lax.fori_loop(0, per_chunk, lambda n, _: group(n, 0, plain, False), 0)
     pl.semaphore_wait(barrier, parts - 1)
+    post(0, 0)
     for f in range(fields):
         slope_of = along_x if f == x_section else plain
         lax.fori_loop(
-            f * per_field,
+            f * per_field if f else per_chunk,
             (f + 1) * per_field,
             lambda n, _, f=f, slope_of=slope_of: group(n, f, slope_of),
             0,
@@ -265,7 +270,8 @@
         return 0
 
     block_rows = shares.shape[1] // parts
-    mine = pl.ds(pl.multiple_of(me * block_rows, 8), block_rows)
+    pitch = got.shape[1] // parts
+    mine = pl.ds(pl.multiple_of(me * pitch, 8), block_rows)
 
     def quarter(h, k):
         q = half * h + k
@@ -293,13 +299,11 @@
         return 0
 
     def give_peaks(h):
-        mine = peak_ref.at[h, chip, core]
-
         def one(i, _):
             to_row, first = chip_at(rem(i * 37, parts // 2))
             pltpu.make_async_remote_copy(
                 src_ref=tops.at[h],
-                dst_ref=mine,
+                dst_ref=got_tops.at[h, chip, core],
                 send_sem=peak_send_sems.at[h],
                 recv_sem=peak_recv_sems.at[h],
                 device_id=(to_row, first + core),
@@ -308,10 +312,10 @@
             return 0
 
         lax.fori_loop(1, parts // 2, one, 0)
-        pltpu.make_async_copy(tops.at[h], mine, peak_own_sems.at[h]).start()
+        got_tops[h, chip, core] = tops[h]
 
     def pair_copy(h):
-        held = peak_ref.at[h, :, core]
+        held = got_tops.at[h, :, core]
         return pltpu.make_async_remote_copy(
             src_ref=held,
             dst_ref=held,
@@ -321,6 +325,42 @@
             device_id_type=pl.DeviceIdType.MESH,
         )
 
+    def hand_over(h):
+        others = got_tops.at[h, pl.ds(0, parts // 2 - 1), 0]
+        pltpu.make_async_copy(others, others, peak_send_sems.at[h]).wait()
+        pltpu.make_async_copy(others, others, peak_recv_sems.at[h]).wait()
+        pair_copy(h).start()
+
+    thick = out_ref.shape[0]
+
+    def put_out(q):
+        return pltpu.make_async_copy(
+            ready.at[q % half], out_ref.at[:, :, pl.ds(q * lanes, lanes)], out_sems.at[q % half]
+        )
+
+    def settle(h):
+        others = got.at[h, pl.ds(0, (parts - 1) * block_rows)]
+        pltpu.make_async_copy(others, others, share_recv_sems.at[h]).wait()
+        for k in range(half):
+            if h:
+                put_out(half * (h - 1) + k).wait()
+            for piece in range(pieces):
+                for plane in range(thick):
+                    at = pl.ds((k * pieces + piece) * thick + plane, parts, stride=pitch)
+                    ready[k, plane, piece * lanes : (piece + 1) * lanes, :] = got[h, at, :].T
+            put_out(half * h + k).start()
+
+    def settle_tops():
+        for h in range(2):
+            pair_copy(h).wait()
+            flat = got_tops.at[h].reshape(parts * half * pieces, lanes)
+            for k in range(half):
+                for piece in range(pieces):
+                    at = pl.ds(k * pieces + piece, parts, stride=half * pieces)
+                    xs = slice((half * h + k) * lanes, (half * h + k + 1) * lanes)
+                    ready_tops[piece * lanes : (piece + 1) * lanes, xs] = flat[at, :].T
+
+    out_tops = pltpu.make_async_copy(ready_tops, peak_ref, out_tops_sem)
     for h in range(2):
         arrived(2 * h)
         lax.fori_loop(0, zblocks, lambda c, _, h=h: on_half(h, c), 0)
@@ -332,28 +372,27 @@
         to_all(
             lambda part, h=h: (
                 shares.at[h, pl.ds(pl.multiple_of(part * block_rows, 8), block_rows)],
-                out_ref.at[h, mine],
+                got.at[h, mine],
                 share_send_sems.at[h],
                 share_recv_sems.at[h],
             )
         )
-        pltpu.make_async_copy(shares.at[h, mine], out_ref.at[h, mine], own_sem.at[h]).start()
-
-    for h in range(2):
-        others = peak_ref.at[h, pl.ds(0, parts // 2 - 1), 0]
-        pltpu.make_async_copy(tops.at[h], peak_ref.at[h, chip, core], peak_own_sems.at[h]).wait()
-        pltpu.make_async_copy(others, others, peak_send_sems.at[h]).wait()
-        pltpu.make_async_copy(others, others, peak_recv_sems.at[h]).wait()
-        pair_copy(h).start()
+        got[h, mine, :] = shares[h, pl.ds(pl.multiple_of(me * block_rows, 8), block_rows), :]
+
+    hand_over(0)
+    settle(0)
+    hand_over(1)
+    settle_tops()
+    out_tops.start()
     sent = send.at[:, pl.ds(0, (parts - 1) * chunk)]
     pltpu.make_async_copy(sent, sent, send_sem).wait()
     for h in range(2):
-        pair_copy(h).wait()
-        others = out_ref.at[h, pl.ds(0, (parts - 1) * block_rows)]
-        own = out_ref.at[h, pl.ds(0, block_rows)]
-        pltpu.make_async_copy(own, own, own_sem.at[h]).wait()
+        others = shares.at[h, pl.ds(0, (parts - 1) * block_rows)]
         pltpu.make_async_copy(others, others, share_send_sems.at[h]).wait()
-        pltpu.make_async_copy(others, others, share_recv_sems.at[h]).wait()
+    settle(1)
+    for k in range(half):
+        put_out(half + k).wait()
+    out_tops.wait()
 
 
 def fused(velocity, high, low, sizes, old_place, new_col, parts):
@@ -374,8 +413,8 @@
         in_specs=[anywhere, vmem, vmem, smem, smem, smem],
         out_specs=[anywhere, anywhere],
         out_shape=[
-            jax.ShapeDtypeStruct((2, parts * block_rows, lanes), jnp.float32),
-            jax.ShapeDtypeStruct((2, parts // 2, 2, 8, lanes), jnp.float32),
+            jax.ShapeDtypeStruct((4, height, width), jnp.float32),
+            jax.ShapeDtypeStruct((height, width), jnp.float32),
         ],
         scratch_shapes=[
             pltpu.VMEM((3, 8, planes, width), jnp.float32),
@@ -392,6 +431,10 @@
             pltpu.VMEM((height * height // lanes, lanes), jnp.float32),
             pltpu.VMEM((2, parts * block_rows, lanes), jnp.float32),
             pltpu.VMEM((2, 8, lanes), jnp.float32),
+            pltpu.VMEM((2, parts * 40, lanes), jnp.float32),
+            pltpu.VMEM((2, parts // 2, 2, 8, lanes), jnp.float32),
+            pltpu.VMEM((2, 4, height, lanes), jnp.float32),
+            pltpu.VMEM((height, width), jnp.float32),
             pltpu.SMEM((blocks,), jnp.int32),
             pltpu.SMEM((height // 4,), jnp.int32),
             pltpu.SMEM((zblocks * 3 * height // 8,), jnp.int32),
@@ -400,7 +443,8 @@
             pltpu.SemaphoreType.DMA,
             pltpu.SemaphoreType.DMA((3,)),
         ]
-        + [pltpu.SemaphoreType.DMA((2,))] * 8,
+        + [pltpu.SemaphoreType.DMA((2,))] * 7
+        + [pltpu.SemaphoreType.DMA],
         compiler_params=pltpu.CompilerParams(
             vmem_limit_bytes=63 << 20, has_side_effects=True, collective_id=0
         ),
@@ -411,48 +455,11 @@
     )(velocity, high, low, sizes, old_place, new_col)
 
 
-def finish_kernel(g_ref, p_ref, out_ref, peak_ref):
-    thick, height, parts = out_ref.shape
-    rows, lanes = g_ref.shape[1] // parts, g_ref.shape[2]
-    chunks = height // lanes
-    k = pl.program_id(0) % 2
-    for chunk in range(chunks):
-        ys = slice(chunk * lanes, (chunk + 1) * lanes)
-        for plane in range(thick):
-            at = pl.ds((k * chunks + chunk) * thick + plane, parts, stride=rows)
-            out_ref[plane, ys, :] = g_ref[0, at, :].T
-        tops = pl.ds(k * chunks + chunk, parts, stride=2 * chunks)
-        peak_ref[ys, :] = p_ref[0, tops, :].T
-
-
-def finish(received, tops, parts, thick, height):
-    quarters = height // parts
-    return pl.pallas_call(
-        finish_kernel,
-        grid=(quarters,),
-        in_specs=[
-            pl.BlockSpec((1,) + received.shape[1:], lambda q: (q // 2, 0, 0)),
-            pl.BlockSpec((1,) + tops.shape[1:], lambda q: (q // 2, 0, 0)),
-        ],
-        out_specs=[
-            pl.BlockSpec((thick, height, parts), lambda q: (0, 0, q)),
-            pl.BlockSpec((height, parts), lambda q: (0, q)),
-        ],
-        out_shape=[
-            jax.ShapeDtypeStruct((thick, height, quarters * parts), jnp.float32),
-            jax.ShapeDtypeStruct((height, quarters * parts), jnp.float32),
-        ],
-        compiler_params=pltpu.CompilerParams(vmem_limit_bytes=32 << 20),
-        cost_estimate=pl.CostEstimate(flops=1 << 20, bytes_accessed=10 << 20, transcendentals=0),
-        name="finish",
-    )(received, tops)
-
-
 def on_device(velocity, y_sizes, old_place, new_col):
     fields, _, places, depth, planes, width = velocity.shape
     parts = lax.axis_size("row") * lax.axis_size("col")
     high, low = two_halves(spectral_matrix(width))
-    received, tops = fused(
+    field, peak = fused(
         velocity.reshape(fields, places * depth, planes, width),
         high,
         low,
@@ -461,8 +468,6 @@
         new_col,
         parts,
     )
-    tops = tops.reshape(2, parts * 8, parts)
-    field, peak = finish(received, tops, parts, 4, width)
     return field.reshape(2, 1, 2, width, width), peak
 
 

time: 228 us -> 226 us (level)
  Pallas kernels: 224 us -> 219 us
  local copies, waits for them, and re-layouts: 3.41 us -> 5.7 us
    pallas_call x1 -> x0, Pallas kernels: 4.41 us -> none  [finish(): pl.pallas_call(finish_kernel, grid=(quarters,), in_specs=[pl.BlockSpec((1...]
    unnamed x4, local copies, waits for them, and re-layouts: 3.41 us -> 5.7 us
where the time goes in v6:
time: 226 us
  Pallas kernels  219 us (97%)
  local copies, waits for them, and re-layouts  5.7 us (3%)
    pallas_call x1, Pallas kernels, fused(): pl.pallas_call(fused_kernel, in_specs=[anywhere, vmem, vmem, smem, smem,...  219 us
    unnamed x4, local copies, waits for them, and re-layouts  5.7 us

profile of v6, /device:TPU:1, one launch (start us, length us, event | category | flops | bytes accessed | tf_op | source)
XLA Modules:
  0.0 225.6 jit_solution(5094054876316901874)
XLA Ops:
  0.6 219.3 %fused.1 = (f32[4,512,512]{2,1,0:T(8,128)}, f32[512,512]{1,0:T(8,128)}) custom-call(f32[3,72,32,512]{3,2,1,0:T(8,128)} %bitcast.5, bf16[512,512]{1,0:T(8,128)(2,1)} %constant.4.clone.high_ref, bf16[512,512]{1,0:T(8,128)(2,1)} %constant.5.clone.low_ref, s32[16]{0:T(128)} %sizes_ref.1, s32[16,16]{1,0:T(8,128)} %place_ref.1, s32[16,16]{1,0:T(8,128)} %col_ref.1), custom_call_target="tpu_custom_call" | custom-call | flops 7247757312 | bytes 33554432 | tf_op jit(solution)/shard_map/fused/pallas_call | solution.py:411
  219.9 0.0 copy-start
  219.9 4.7 %copy.11 = f32[2,1,2,512,512]{4,3,2,1,0:T(8,128)} copy(f32[2,1,2,512,512]{4,3,2,1,0:T(8,128)} %bitcast.4) | data formatting | bytes 8388608
  224.7 0.0 copy-done
  224.7 1.0 copy.12
Async XLA Ops:
  219.9 4.7 %copy-start = (f32[512,512]{1,0:T(8,128)S(1)}, f32[512,512]{1,0:T(8,128)}, u32[]{:S(2)}) copy-start(f32[512,512]{1,0:T(8,128)} %get-tuple-element.11) | copy-start | bytes 3145732

commit v7 on v6

--- a/solution.py
+++ b/solution.py
@@ -1,3 +1,4 @@
+import functools
 import math
 
 import jax
@@ -33,12 +34,12 @@
 
 
 def fused_kernel(
-    v_ref, high_ref, low_ref, sizes_ref, place_ref, col_ref, out_ref, peak_ref,
+    v_ref, high_ref, low_ref, sizes_ref, place_ref, col_ref, out_ref, late_ref, peak_ref,
     stage, send, in_a, in_x, in_b, aligned, z_high, z_low, y_high, y_low, total, field, shares,
     tops, got, got_tops, ready, ready_tops,
     ends, bounds, source, slab_of,
     in_sems, send_sem, recv_sems, share_send_sems, share_recv_sems,
-    peak_send_sems, peak_recv_sems, pair_send_sems, pair_recv_sems, out_sems, out_tops_sem,
+    peak_send_sems, peak_recv_sems, pair_send_sems, pair_recv_sems, out_sems, out_tops_sem, own_sem,
 ):
     fields, rows, planes, width = v_ref.shape
     lanes = send.shape[2]
@@ -270,7 +271,8 @@
         return 0
 
     block_rows = shares.shape[1] // parts
-    pitch = got.shape[1] // parts
+    pitch = got.shape[0] // parts
+    landing = (got, late_ref)
     mine = pl.ds(pl.multiple_of(me * pitch, 8), block_rows)
 
     def quarter(h, k):
@@ -335,20 +337,21 @@
 
     def put_out(q):
         return pltpu.make_async_copy(
-            ready.at[q % half], out_ref.at[:, :, pl.ds(q * lanes, lanes)], out_sems.at[q % half]
-        )
-
-    def settle(h):
-        others = got.at[h, pl.ds(0, (parts - 1) * block_rows)]
+            ready.at[q], out_ref.at[:, :, pl.ds(q * lanes, lanes)], out_sems.at[q]
+        )
+
+    def all_landed(h):
+        others = landing[h].at[pl.ds(0, (parts - 1) * block_rows)]
         pltpu.make_async_copy(others, others, share_recv_sems.at[h]).wait()
+
+    def settle_first():
+        all_landed(0)
         for k in range(half):
-            if h:
-                put_out(half * (h - 1) + k).wait()
             for piece in range(pieces):
                 for plane in range(thick):
                     at = pl.ds((k * pieces + piece) * thick + plane, parts, stride=pitch)
-                    ready[k, plane, piece * lanes : (piece + 1) * lanes, :] = got[h, at, :].T
-            put_out(half * h + k).start()
+                    ready[k, plane, piece * lanes : (piece + 1) * lanes, :] = got[at, :].T
+            put_out(k).start()
 
     def settle_tops():
         for h in range(2):
@@ -372,15 +375,20 @@
         to_all(
             lambda part, h=h: (
                 shares.at[h, pl.ds(pl.multiple_of(part * block_rows, 8), block_rows)],
-                got.at[h, mine],
+                landing[h].at[mine],
                 share_send_sems.at[h],
                 share_recv_sems.at[h],
             )
         )
-        got[h, mine, :] = shares[h, pl.ds(pl.multiple_of(me * block_rows, 8), block_rows), :]
+        kept = pl.ds(pl.multiple_of(me * block_rows, 8), block_rows)
+        if h == 0:
+            got[mine, :] = shares[h, kept, :]
+        else:
+            own = pltpu.make_async_copy(shares.at[h, kept], late_ref.at[mine], own_sem)
+            own.start()
 
     hand_over(0)
-    settle(0)
+    settle_first()
     hand_over(1)
     settle_tops()
     out_tops.start()
@@ -389,10 +397,11 @@
     for h in range(2):
         others = shares.at[h, pl.ds(0, (parts - 1) * block_rows)]
         pltpu.make_async_copy(others, others, share_send_sems.at[h]).wait()
-    settle(1)
     for k in range(half):
-        put_out(half + k).wait()
+        put_out(k).wait()
     out_tops.wait()
+    own.wait()
+    all_landed(1)
 
 
 def fused(velocity, high, low, sizes, old_place, new_col, parts):
@@ -411,9 +420,10 @@
     return pl.pallas_call(
         fused_kernel,
         in_specs=[anywhere, vmem, vmem, smem, smem, smem],
-        out_specs=[anywhere, anywhere],
+        out_specs=[anywhere, anywhere, anywhere],
         out_shape=[
-            jax.ShapeDtypeStruct((4, height, width), jnp.float32),
+            jax.ShapeDtypeStruct((4, height, width // 2), jnp.float32),
+            jax.ShapeDtypeStruct((parts * 40, lanes), jnp.float32),
             jax.ShapeDtypeStruct((height, width), jnp.float32),
         ],
         scratch_shapes=[
@@ -431,7 +441,7 @@
             pltpu.VMEM((height * height // lanes, lanes), jnp.float32),
             pltpu.VMEM((2, parts * block_rows, lanes), jnp.float32),
             pltpu.VMEM((2, 8, lanes), jnp.float32),
-            pltpu.VMEM((2, parts * 40, lanes), jnp.float32),
+            pltpu.VMEM((parts * 40, lanes), jnp.float32),
             pltpu.VMEM((2, parts // 2, 2, 8, lanes), jnp.float32),
             pltpu.VMEM((2, 4, height, lanes), jnp.float32),
             pltpu.VMEM((height, width), jnp.float32),
@@ -444,7 +454,7 @@
             pltpu.SemaphoreType.DMA((3,)),
         ]
         + [pltpu.SemaphoreType.DMA((2,))] * 7
-        + [pltpu.SemaphoreType.DMA],
+        + [pltpu.SemaphoreType.DMA] * 2,
         compiler_params=pltpu.CompilerParams(
             vmem_limit_bytes=63 << 20, has_side_effects=True, collective_id=0
         ),
@@ -455,11 +465,49 @@
     )(velocity, high, low, sizes, old_place, new_col)
 
 
+def finish_kernel(first_ref, late_ref, top_ref, out_ref, peak_ref, *, parts):
+    plane = pl.program_id(0)
+    thick = pl.num_programs(0)
+    done, lanes = first_ref.shape[2], late_ref.shape[1]
+    pieces = first_ref.shape[1] // lanes
+    out_ref[0, :, :done] = first_ref[0]
+    peak_ref[...] = top_ref[...]
+    for k in range((out_ref.shape[2] - done) // parts):
+        for piece in range(pieces):
+            start = (k * pieces + piece) * thick + plane
+            at = pl.ds(start, parts, stride=late_ref.shape[0] // parts)
+            xs = slice(done + k * parts, done + (k + 1) * parts)
+            out_ref[0, piece * lanes : (piece + 1) * lanes, xs] = late_ref[at, :].T
+
+
+def finish(first, late, top, parts):
+    thick, height, done = first.shape
+    width = top.shape[1]
+    tops = pl.BlockSpec((height // thick, width), lambda p: (p, 0))
+    return pl.pallas_call(
+        functools.partial(finish_kernel, parts=parts),
+        grid=(thick,),
+        in_specs=[
+            pl.BlockSpec((1, height, done), lambda p: (p, 0, 0)),
+            pl.BlockSpec(late.shape, lambda p: (0, 0)),
+            tops,
+        ],
+        out_specs=[pl.BlockSpec((1, height, width), lambda p: (p, 0, 0)), tops],
+        out_shape=[
+            jax.ShapeDtypeStruct((thick, height, width), jnp.float32),
+            jax.ShapeDtypeStruct(top.shape, jnp.float32),
+        ],
+        compiler_params=pltpu.CompilerParams(vmem_limit_bytes=63 << 20),
+        cost_estimate=pl.CostEstimate(flops=1 << 20, bytes_accessed=10 << 20, transcendentals=0),
+        name="finish",
+    )(first, late, top)
+
+
 def on_device(velocity, y_sizes, old_place, new_col):
     fields, _, places, depth, planes, width = velocity.shape
     parts = lax.axis_size("row") * lax.axis_size("col")
     high, low = two_halves(spectral_matrix(width))
-    field, peak = fused(
+    first, late, peak = fused(
         velocity.reshape(fields, places * depth, planes, width),
         high,
         low,
@@ -468,6 +516,7 @@
         new_col,
         parts,
     )
+    field, peak = finish(first, late, peak, parts)
     return field.reshape(2, 1, 2, width, width), peak
 
 

time: 226 us -> 224 us (level)
  local copies, waits for them, and re-layouts: 5.7 us -> 0 us
  Pallas kernels: 219 us -> 223 us
    pallas_call x0 -> x1, Pallas kernels: none -> 5.78 us  [finish(): pl.pallas_call(functools.partial(finish_kernel, parts=parts), grid=(thick...]
    unnamed x4 -> x0, local copies, waits for them, and re-layouts: 5.7 us -> none
where the time goes in v7:
time: 224 us
  Pallas kernels  223 us (100%)
    pallas_call x1, Pallas kernels, fused(): pl.pallas_call(fused_kernel, in_specs=[anywhere, vmem, vmem, smem, smem,...  218 us
    pallas_call x1, Pallas kernels, finish(): pl.pallas_call(functools.partial(finish_kernel, parts=parts), grid=(thick...  5.78 us

profile of v7, /device:TPU:1, one launch (start us, length us, event | category | flops | bytes accessed | tf_op | source)
XLA Modules:
  0.0 224.1 jit_solution(16347616134991353174)
XLA Ops:
  0.6 217.6 %fused.1 = (f32[4,512,256]{2,1,0:T(8,128)}, f32[5120,128]{1,0:T(8,128)}, f32[512,512]{1,0:T(8,128)}) custom-call(f32[3,72,32,512]{3,2,1,0:T(8,128)} %bitcast.4, bf16[512,512]{1,0:T(8,128)(2,1)} %constant.4.clone.high_ref, bf16[512,512]{1,0:T(8,128)(2,1)} %constant.5.clone.low_ref, s32[16]{0:T(128)} %sizes_ref.1, s32[16,16]{1,0:T(8,128)} %place_ref.1, ...), custom_call_target="tpu_custom_call" | custom-call | flops 7247757312 | bytes 33554432 | tf_op jit(solution)/shard_map/fused/pallas_call | solution.py:420
  218.3 5.8 %finish.1 = (f32[4,512,512]{2,1,0:T(8,128)}, f32[512,512]{1,0:T(8,128)}) custom-call(f32[4,512,256]{2,1,0:T(8,128)} %get-tuple-element.7.first_ref, f32[5120,128]{1,0:T(8,128)} %get-tuple-element.8.late_ref, f32[512,512]{1,0:T(8,128)} %get-tuple-element.9.top_ref), custom_call_target="tpu_custom_call" | custom-call | flops 1048576 | bytes 10485760 | tf_op jit(solution)/shard_map/finish/pallas_call | solution.py:487

commit v8 on v7

--- a/solution.py
+++ b/solution.py
@@ -34,11 +34,11 @@
 
 
 def fused_kernel(
-    v_ref, high_ref, low_ref, sizes_ref, place_ref, col_ref, out_ref, late_ref, peak_ref,
-    stage, send, in_a, in_x, in_b, aligned, z_high, z_low, y_high, y_low, total, field, shares,
+    v_ref, high_hbm, low_hbm, sizes_ref, place_ref, col_ref, out_ref, late_ref, peak_ref,
+    high_ref, low_ref, stage, send, in_a, in_x, in_b, aligned, z_high, z_low, y_high, y_low, total, field, shares,
     tops, got, got_tops, ready, ready_tops,
     ends, bounds, source, slab_of,
-    in_sems, send_sem, recv_sems, share_send_sems, share_recv_sems,
+    matrix_sems, in_sems, send_sem, recv_sems, share_send_sems, share_recv_sems,
     peak_send_sems, peak_recv_sems, pair_send_sems, pair_recv_sems, out_sems, out_tops_sem, own_sem,
 ):
     fields, rows, planes, width = v_ref.shape
@@ -181,14 +181,23 @@
         slope = dot(high, high_ref[...]) + (dot(high, low_ref[...]) + dot(low, high_ref[...]))
         return lambda r: -slope[r * planes : (r + 1) * planes]
 
-    lax.fori_loop(1, parts, greet, 0)
     for n in range(slots):
         start_load(0, n)
+    matrix = [
+        pltpu.make_async_copy(high_hbm, high_ref, matrix_sems.at[0]),
+        pltpu.make_async_copy(low_hbm, low_ref, matrix_sems.at[1]),
+    ]
+    for copy in matrix:
+        copy.start()
+    lax.fori_loop(1, parts, greet, 0)
     lax.fori_loop(0, per_chunk, lambda n, _: group(n, 0, plain, False), 0)
     pl.semaphore_wait(barrier, parts - 1)
     post(0, 0)
     for f in range(fields):
         slope_of = along_x if f == x_section else plain
+        if f == x_section:
+            for copy in matrix:
+                copy.wait()
         lax.fori_loop(
             f * per_field if f else per_chunk,
             (f + 1) * per_field,
@@ -412,14 +421,13 @@
     quarters = width // parts
     zblocks, blocks = old_place.shape
     block_rows = 32
-    vmem = pl.BlockSpec(memory_space=pltpu.VMEM)
     smem = pl.BlockSpec(memory_space=pltpu.SMEM)
     anywhere = pl.BlockSpec(memory_space=pl.ANY)
     arrival = pltpu.VMEM((parts * rows + 16, lanes), jnp.float32)
     operand = pltpu.VMEM((quarters, height, height), jnp.bfloat16)
     return pl.pallas_call(
         fused_kernel,
-        in_specs=[anywhere, vmem, vmem, smem, smem, smem],
+        in_specs=[anywhere, anywhere, anywhere, smem, smem, smem],
         out_specs=[anywhere, anywhere, anywhere],
         out_shape=[
             jax.ShapeDtypeStruct((4, height, width // 2), jnp.float32),
@@ -427,6 +435,8 @@
             jax.ShapeDtypeStruct((height, width), jnp.float32),
         ],
         scratch_shapes=[
+            pltpu.VMEM((height, height), jnp.bfloat16),
+            pltpu.VMEM((height, height), jnp.bfloat16),
             pltpu.VMEM((3, 8, planes, width), jnp.float32),
             pltpu.VMEM((fields * rows // chunk, parts * chunk, lanes), jnp.float32),
             arrival,
@@ -449,6 +459,7 @@
             pltpu.SMEM((height // 4,), jnp.int32),
             pltpu.SMEM((zblocks * 3 * height // 8,), jnp.int32),
             pltpu.SMEM((zblocks * new_col.shape[1],), jnp.int32),
+            pltpu.SemaphoreType.DMA((2,)),
             pltpu.SemaphoreType.DMA((3, 2)),
             pltpu.SemaphoreType.DMA,
             pltpu.SemaphoreType.DMA((3,)),

time: 224 us -> 224 us (level)
  no operation moved by 1% of the time
where the time goes in v8:
time: 224 us
  Pallas kernels  223 us (100%)
    pallas_call x1, Pallas kernels, fused(): pl.pallas_call(fused_kernel, in_specs=[anywhere, anywhere, anywhere, smem...  217 us
    pallas_call x1, Pallas kernels, finish(): pl.pallas_call(functools.partial(finish_kernel, parts=parts), grid=(thick...  5.78 us

profile of v8, /device:TPU:1, one launch (start us, length us, event | category | flops | bytes accessed | tf_op | source)
XLA Modules:
  0.0 223.8 jit_solution(17380651126670698564)
XLA Ops:
  0.6 217.4 %fused.1 = (f32[4,512,256]{2,1,0:T(8,128)}, f32[5120,128]{1,0:T(8,128)}, f32[512,512]{1,0:T(8,128)}) custom-call(f32[3,72,32,512]{3,2,1,0:T(8,128)} %bitcast.4, bf16[512,512]{1,0:T(8,128)(2,1)} %constant.4.clone.high_hbm, bf16[512,512]{1,0:T(8,128)(2,1)} %constant.5.clone.low_hbm, s32[16]{0:T(128)} %sizes_ref.1, s32[16,16]{1,0:T(8,128)} %place_ref.1, ...), custom_call_target="tpu_custom_call" | custom-call | flops 7247757312 | bytes 33554432 | tf_op jit(solution)/shard_map/fused/pallas_call | solution.py:428
  218.0 5.8 %finish.1 = (f32[4,512,512]{2,1,0:T(8,128)}, f32[512,512]{1,0:T(8,128)}) custom-call(f32[4,512,256]{2,1,0:T(8,128)} %get-tuple-element.7.first_ref, f32[5120,128]{1,0:T(8,128)} %get-tuple-element.8.late_ref, f32[512,512]{1,0:T(8,128)} %get-tuple-element.9.top_ref), custom_call_target="tpu_custom_call" | custom-call | flops 1048576 | bytes 10485760 | tf_op jit(solution)/shard_map/finish/pallas_call | solution.py:498
